TPU v7x, 256 devices: a whole 4x4x8 slice. The times are simulated.
256 devices in a mesh: tm: 32 (over z, y), sx: 4 (over x), sy: 2 (over core).
Axes of the slice: x: 4, y: 4, z: 8, core: 2. Of those that a mesh axis runs over, the one named last changes fastest.
Arguments:
- thickness_guess: float32 [32, 1024, 256], P('tm', 'sx', 'sy'), may hold values from 0.5 to 1.5
- thickness_start: float32 [1024, 256], P('sx', 'sy'), may hold values from 0.5 to 1.5
- bed: float32 [1024, 256], P('sx', 'sy'), may hold values from -1.8 to 1.8
- rate_factor: float32 [1024, 256], P('sx', 'sy'), may hold values from 0.05 to 0.5
- mass_balance: float32 [32, 1024, 256], P('tm', 'sx', 'sy'), may hold values from -1.2 to 1.2
- cell_flags: int32 [1024, 256], P('sx', 'sy'), may hold values from 0 to 2, as said below
Outputs:
- thickness: float32 [32, 1024, 256], P('tm', 'sx', 'sy')
Inputs may be any that keep to these rules, and one draw needn't show every extreme that they name: `cell_flags`: 0 marks ice-free cells outside the glacier, 1 ice on bedrock, 2 ice on soft sediment.
All inputs are finite; a program needn't handle non-finite values.
Results may differ from a plain program's by a relative error of at most 0.00015.
Values sent between devices are 32-bit elements; how exact they have to be, the bound alone decides.
A program may use at most 64 MiB of HBM per device.

v0:
```python
import math

import jax
import jax.numpy as jnp
from jax import lax
from jax.sharding import PartitionSpec as P

NEWTON = 2
SWEEPS = 8


circulant_weight = 0.25
time_step = 1.0
precise = lax.Precision.HIGHEST


def from_behind(value, axis, steps):
    count = lax.axis_size(axis)
    initial, last = (max(0, -steps), min(count, count - steps))
    return lax.ppermute(value, axis, [(source, source + steps) for source in range(initial, last)])


def padded_2(array, sides, width):
    edges = {}
    for axis, dim in sides:
        peers, length = (lax.axis_size(axis), array.shape[dim])
        up = [(i, (i + 1) % peers) for i in range(peers - 1)]
        last = lax.slice_in_dim(array, length - width, length, axis=dim)
        initial = lax.slice_in_dim(array, 0, width, axis=dim)
        edges[dim] = (
            lax.ppermute(last, axis, up),
            lax.ppermute(initial, axis, [(b, a) for a, b in up]),
        )
    done = []
    for _, dim in sides:
        low, high = edges[dim]
        around = [(width, width) if d in done else (0, 0) for d in range(array.ndim)]
        array = jnp.concatenate([jnp.pad(low, around), array, jnp.pad(high, around)], axis=dim)
        done.append(dim)
    return array


def from_everyone(array, axis):
    peers = lax.axis_size(axis)
    return lax.all_to_all(
        jnp.broadcast_to(array[None], (peers, *array.shape)), axis, 0, 0, tiled=True
    )


def taken_together(array, axis):
    return from_everyone(array, axis).sum(axis=0)


def extended(block, sides, width):
    for axis, dim in sides:
        count = lax.axis_size(axis)
        forward = [(i, i + 1) for i in range(count - 1)]
        backward = [(target, source) for source, target in forward]
        low = lax.ppermute(
            lax.slice_in_dim(block, block.shape[dim] - width, None, axis=dim), axis, forward
        )
        high = lax.ppermute(lax.slice_in_dim(block, 0, width, axis=dim), axis, backward)
        block = jnp.concatenate([low, block, high], axis=dim)
    return block


def cell_diffusivity(thickness, rate_factor, cell_flags):
    inside = (cell_flags != 0).astype(jnp.float32)
    boost = 1.0 + (cell_flags == 2).astype(jnp.float32)
    return inside * boost * rate_factor * thickness * thickness * jnp.abs(thickness)


def face_weights(padded):
    centre = padded[1:-1, 1:-1]
    return (
        0.5 * (centre + padded[2:, 1:-1]),
        0.5 * (centre + padded[:-2, 1:-1]),
        0.5 * (centre + padded[1:-1, 2:]),
        0.5 * (centre + padded[1:-1, :-2]),
    )


def neighbour_sum(weights, padded):
    return (
        weights[0] * padded[2:, 1:-1]
        + weights[1] * padded[:-2, 1:-1]
        + weights[2] * padded[1:-1, 2:]
        + weights[3] * padded[1:-1, :-2]
    )


def dft_tables(level_count):
    row_index = lax.broadcasted_iota(jnp.int32, (level_count, level_count), 0)
    col_index = lax.broadcasted_iota(jnp.int32, (level_count, level_count), 1)
    phase = 2.0 * math.pi / level_count * (row_index * col_index % level_count).astype(jnp.float32)
    return (jnp.cos(phase), jnp.sin(phase))


def forward_block(pieces):
    cosine, sine_table = dft_tables(pieces.shape[0])
    real_part = jnp.einsum("kl,lrc->krc", cosine, pieces, precision=precise)
    imag_part = -jnp.einsum("kl,lrc->krc", sine_table, pieces, precision=precise)
    return lax.all_to_all(
        jnp.stack([real_part, imag_part]), "tm", split_axis=1, concat_axis=2, tiled=True
    )


def inverse_block(pieces):
    level_count = pieces.shape[1]
    cosine, sine_table = dft_tables(level_count)
    values = (
        jnp.einsum("lk,krc->lrc", cosine, pieces[0], precision=precise)
        - jnp.einsum("lk,krc->lrc", sine_table, pieces[1], precision=precise)
    ) / level_count
    return lax.all_to_all(values, "tm", split_axis=0, concat_axis=1, tiled=True)


def window(matrix, offset, row_count, col_count):
    return matrix[offset : offset + row_count, offset : offset + col_count]


def jacobi_sweeps(source_wide, weights, coeffs, depth, row_count, col_count, grow):
    margin = depth
    value_real = source_wide[0] * coeffs[0] + source_wide[1] * coeffs[1]
    value_imag = source_wide[0] * coeffs[2] + source_wide[1] * coeffs[3]
    for sweep_index in range(SWEEPS - 1):
        if margin == 0:
            grown = grow(jnp.stack([value_real, value_imag]))
            value_real, value_imag = (grown[0], grown[1])
            margin = depth
        inner_margin = margin - 1
        offset = depth - inner_margin
        height = row_count + 2 * inner_margin
        breadth = col_count + 2 * inner_margin
        local_weights = tuple((window(member, offset, height, breadth) for member in weights))
        local_coeffs = tuple((window(member, offset, height, breadth) for member in coeffs))
        numer_real = window(source_wide[0], offset, height, breadth) + neighbour_sum(
            local_weights, value_real
        )
        numer_imag = window(source_wide[1], offset, height, breadth) + neighbour_sum(
            local_weights, value_imag
        )
        value_real = numer_real * local_coeffs[0] + numer_imag * local_coeffs[1]
        value_imag = numer_real * local_coeffs[2] + numer_imag * local_coeffs[3]
        margin = inner_margin
    return (
        window(value_real, margin, row_count, col_count),
        window(value_imag, margin, row_count, col_count),
    )


def body(thickness_guess, thickness_start, bed, rate_factor, mass_balance, cell_flags):
    level_count = lax.axis_size("tm")
    level_index = lax.axis_index("tm")
    depth = 4
    inside = (cell_flags != 0).astype(jnp.float32)
    ratio_root = circulant_weight ** (1.0 / level_count)
    angle = 2.0 * math.pi / level_count * level_index.astype(jnp.float32)
    shift_real = (1.0 - ratio_root * jnp.cos(angle)) / time_step
    shift_imag = ratio_root * jnp.sin(angle) / time_step
    lift_scale = ratio_root ** level_index.astype(jnp.float32)
    thickness = thickness_guess[0]
    balance = mass_balance[0]
    row_count, col_count = thickness.shape
    for newton_step in range(NEWTON):
        prior_level = from_behind(thickness, "tm", 1)
        prior_level = jnp.where(level_index == 0, thickness_start, prior_level)
        diffuse = cell_diffusivity(thickness, rate_factor, cell_flags)
        surface = thickness + bed
        padded = padded_2(jnp.stack([surface, diffuse]), (("sx", 1), ("sy", 2)), 1)
        weights = face_weights(padded[1])
        face_total = weights[0] + weights[1] + weights[2] + weights[3]
        change = (
            (thickness - prior_level) / time_step
            + face_total * surface
            - neighbour_sum(weights, padded[0])
            - balance
        )
        residual = inside * change
        mean_diff = taken_together(diffuse, "tm") / level_count
        mean_rim = extended(jnp.stack([mean_diff, inside]), (("sx", 1), ("sy", 2)), depth + 1)
        mean_weights = face_weights(mean_rim[0])
        mean_total = mean_weights[0] + mean_weights[1] + mean_weights[2] + mean_weights[3]
        inside_wide = mean_rim[1][1:-1, 1:-1]
        denom_real = shift_real + mean_total
        denom_norm = denom_real * denom_real + shift_imag * shift_imag
        inverse_real = inside_wide * denom_real / denom_norm
        inverse_imag = -inside_wide * shift_imag / denom_norm
        source = residual * lift_scale
        spectrum = forward_block(
            lax.all_to_all(source[None], "tm", split_axis=1, concat_axis=0, tiled=True)
        )
        spectrum_real, spectrum_imag = (spectrum[0, 0], spectrum[1, 0])
        source_wide = extended(
            jnp.stack([spectrum_real, spectrum_imag]), (("sx", 1), ("sy", 2)), depth
        )

        def tile_extend(stacked):
            return extended(stacked, (("sx", 1), ("sy", 2)), depth)

        coeffs = (inverse_real, -inverse_imag, inverse_imag, inverse_real)
        solution_real, solution_imag = jacobi_sweeps(
            source_wide, mean_weights, coeffs, depth, row_count, col_count, tile_extend
        )
        update = inverse_block(
            lax.all_to_all(
                jnp.stack([solution_real, solution_imag])[:, None],
                "tm",
                split_axis=2,
                concat_axis=1,
                tiled=True,
            )
        )[0]
        thickness = thickness - update / lift_scale
    return thickness[None]


def solution(mesh):
    in_specs = (
        P("tm", "sx", "sy"),
        P("sx", "sy"),
        P("sx", "sy"),
        P("sx", "sy"),
        P("tm", "sx", "sy"),
        P("sx", "sy"),
    )
    out_specs = P("tm", "sx", "sy")
    return jax.shard_map(body, mesh=mesh, in_specs=in_specs, out_specs=out_specs, check_vma=False)
```

profile of v0, /device:TPU:6, one launch (start us, length us, event | category | flops | bytes accessed | tf_op | source)
XLA Modules:
  0.0 452.0 jit_solution(14615766117768035924)
XLA Ops:
  2.7 3.1 collective-permute-start.1
  5.8 2.7 collective-permute-start.3
  9.8 3.5 collective-permute-start
  16.4 23.2 %all_to_all.88 = f32[1,256,128]{2,0,1:T(1,128)S(1)} all-to-all(f32[1,256,128]{2,0,1:T(1,128)S(1)} %bitcast.178), channel_id=1, replica_groups=mesh['tm'=32,'sx'=4,'sy'=2] {'tm'}, dimensions={1} | all-to-all | bytes 262144 | tf_op jit(solution)/shard_map/all_to_all | solution.py:191
  40.6 14.7 %all_to_all.89 = f32[2,32,8,128]{3,2,0,1:T(8,128)S(1)} all-to-all(f32[2,32,8,128]{3,2,0,1:T(8,128)S(1)} %copy.49), channel_id=1, replica_groups=mesh['tm'=32,'sx'=4,'sy'=2] {'tm'}, dimensions={1} | all-to-all | bytes 524288 | tf_op jit(solution)/shard_map/all_to_all | solution.py:103
  57.9 4.9 %all-to-all-start.2 = ((f32[32,256,128]{2,1,0:T(8,128)}), f32[32,256,128]{2,1,0:T(8,128)}, u32[]{:S(2)}, u32[]{:S(2)}) async-start(f32[32,256,128]{2,1,0:T(8,128)} %broadcast_in_dim.26), calls=%async_computation.2 | async-start | bytes 8388608 | tf_op jit(solution)/shard_map/all_to_all | solution.py:45
  62.8 4.5 collective-permute-start.6
  68.7 4.0 collective-permute-done.5
  74.2 3.1 collective-permute-start.7
  77.3 77.3 %all-to-all-done.2 = f32[32,256,128]{2,1,0:T(8,128)} async-done(((f32[32,256,128]{2,1,0:T(8,128)}), f32[32,256,128]{2,1,0:T(8,128)}, u32[]{:S(2)}, u32[]{:S(2)}) %all-to-all-start.2) | async-done | bytes 4194336 | tf_op jit(solution)/shard_map/all_to_all | solution.py:45
  157.0 4.2 collective-permute-start.10
  162.8 3.9 collective-permute-done.9
  168.2 3.1 collective-permute-start.11
  181.9 4.2 collective-permute-done.13
  187.5 3.2 collective-permute-start.15
  196.1 18.4 %all_to_all.90 = f32[2,1,256,128]{3,0,1,2:T(2,128)S(1)} all-to-all(f32[2,1,256,128]{3,0,1,2:T(2,128)S(1)} %copy.52), channel_id=1, replica_groups=mesh['tm'=32,'sx'=4,'sy'=2] {'tm'}, dimensions={2} | all-to-all | bytes 524288 | tf_op jit(solution)/shard_map/all_to_all | solution.py:206
  215.5 14.1 %all_to_all.91 = f32[32,8,128]{2,1,0:T(8,128)S(1)} all-to-all(f32[32,8,128]{2,1,0:T(8,128)S(1)} %copy.57), channel_id=1, replica_groups=mesh['tm'=32,'sx'=4,'sy'=2] {'tm'}, dimensions={0} | all-to-all | bytes 262144 | tf_op jit(solution)/shard_map/all_to_all | solution.py:115
  231.2 3.1 collective-permute-start.18
  242.8 18.7 %all_to_all.92 = f32[1,256,128]{2,0,1:T(1,128)S(1)} all-to-all(f32[1,256,128]{2,0,1:T(1,128)S(1)} %bitcast.177), channel_id=1, replica_groups=mesh['tm'=32,'sx'=4,'sy'=2] {'tm'}, dimensions={1} | all-to-all | bytes 262144 | tf_op jit(solution)/shard_map/all_to_all | solution.py:191
  262.5 14.8 %all_to_all.93 = f32[2,32,8,128]{3,2,0,1:T(8,128)S(1)} all-to-all(f32[2,32,8,128]{3,2,0,1:T(8,128)S(1)} %copy.61), channel_id=1, replica_groups=mesh['tm'=32,'sx'=4,'sy'=2] {'tm'}, dimensions={1} | all-to-all | bytes 524288 | tf_op jit(solution)/shard_map/all_to_all | solution.py:103
  279.7 4.9 %all-to-all-start.7 = ((f32[32,256,128]{2,1,0:T(8,128)}), f32[32,256,128]{2,1,0:T(8,128)}, u32[]{:S(2)}, u32[]{:S(2)}) async-start(f32[32,256,128]{2,1,0:T(8,128)} %broadcast_in_dim.29), calls=%async_computation.7 | async-start | bytes 8388608 | tf_op jit(solution)/shard_map/all_to_all | solution.py:45
  284.6 4.5 collective-permute-start.23
  290.4 4.2 collective-permute-done.22
  296.1 3.1 collective-permute-start.24
  299.1 77.3 %all-to-all-done.7 = f32[32,256,128]{2,1,0:T(8,128)} async-done(((f32[32,256,128]{2,1,0:T(8,128)}), f32[32,256,128]{2,1,0:T(8,128)}, u32[]{:S(2)}, u32[]{:S(2)}) %all-to-all-start.7) | async-done | bytes 4194336 | tf_op jit(solution)/shard_map/all_to_all | solution.py:45
  378.9 4.2 collective-permute-start.27
  384.7 3.9 collective-permute-done.26
  390.1 3.3 collective-permute-start.28
  403.5 4.2 collective-permute-done.30
  409.2 3.1 collective-permute-start.32
  417.8 18.5 %all_to_all.94 = f32[2,1,256,128]{3,0,1,2:T(2,128)S(1)} all-to-all(f32[2,1,256,128]{3,0,1,2:T(2,128)S(1)} %copy.64), channel_id=1, replica_groups=mesh['tm'=32,'sx'=4,'sy'=2] {'tm'}, dimensions={2} | all-to-all | bytes 524288 | tf_op jit(solution)/shard_map/all_to_all | solution.py:206
  437.2 14.1 %all_to_all.95 = f32[32,8,128]{2,1,0:T(8,128)S(1)} all-to-all(f32[32,8,128]{2,1,0:T(8,128)S(1)} %copy.69), channel_id=1, replica_groups=mesh['tm'=32,'sx'=4,'sy'=2] {'tm'}, dimensions={0} | all-to-all | bytes 262144 | tf_op jit(solution)/shard_map/all_to_all | solution.py:115
  (167 shorter events, 77.1 us)
Async XLA Ops:
  1.4 12.6 %collective-permute-start.4 = (f32[2,256,1]{2,1,0:T(8,128)S(1)}, f32[2,256,1]{2,1,0:T(8,128)S(1)}, u32[]{:S(2)}, u32[]{:S(2)}) collective-permute-start(f32[2,256,1]{2,1,0:T(8,128)S(1)} %get-tuple-element.132), channel_id=1, source_target_pairs={{1,0},{3,2},{5,4},{7,6},{9,8},{11,10},{13,12},{15,14},{17,16},{19,... | collective-permute-start | bytes 6152 | tf_op jit(solution)/shard_map/ppermute | solution.py:32
  2.7 11.3 %collective-permute-start.1 = (f32[2,256,1]{2,1,0:T(8,128)S(1)}, f32[2,256,1]{2,1,0:T(8,128)S(1)}, u32[]{:S(2)}, u32[]{:S(2)}) collective-permute-start(f32[2,256,1]{2,1,0:T(8,128)S(1)} %get-tuple-element.131), channel_id=1, source_target_pairs={{0,1},{2,3},{4,5},{6,7},{8,9},{10,11},{12,13},{14,15},{16,17},{18,... | collective-permute-start | bytes 6152 | tf_op jit(solution)/shard_map/ppermute | solution.py:31
  5.8 7.6 %collective-permute-start.3 = (f32[2,1,128]{2,1,0:T(1,128)S(1)}, f32[2,1,128]{2,1,0:T(1,128)S(1)}, u32[]{:S(2)}, u32[]{:S(2)}) collective-permute-start(f32[2,1,128]{2,1,0:T(1,128)S(1)} %get-tuple-element.130), channel_id=1, source_target_pairs={{2,0},{4,2},{6,4},{3,1},{5,3},{7,5},{10,8},{12,10},{14,12},{11,9},... | collective-permute-start | bytes 3080 | tf_op jit(solution)/shard_map/ppermute | solution.py:32
  8.5 5.5 %collective-permute-start.2 = (f32[2,1,128]{2,1,0:T(1,128)S(1)}, f32[2,1,128]{2,1,0:T(1,128)S(1)}, u32[]{:S(2)}, u32[]{:S(2)}) collective-permute-start(f32[2,1,128]{2,1,0:T(1,128)S(1)} %get-tuple-element.129), channel_id=1, source_target_pairs={{0,2},{2,4},{4,6},{1,3},{3,5},{5,7},{8,10},{10,12},{12,14},{9,11},... | collective-permute-start | bytes 3080 | tf_op jit(solution)/shard_map/ppermute | solution.py:31
  9.8 6.3 %collective-permute-start = (f32[256,128]{1,0:T(8,128)}, f32[256,128]{1,0:T(8,128)S(1)}, u32[]{:S(2)}, u32[]{:S(2)}) collective-permute-start(f32[256,128]{1,0:T(8,128)} %bitcast.172), channel_id=1, source_target_pairs={{0,8},{8,16},{16,24},{24,32},{32,40},{40,48},{48,56},{56,64},{64,7... | collective-permute-start | bytes 393224 | tf_op jit(solution)/shard_map/ppermute | solution.py:20
  57.9 96.7 %all-to-all-start.2 = ((f32[32,256,128]{2,1,0:T(8,128)}), f32[32,256,128]{2,1,0:T(8,128)}, u32[]{:S(2)}, u32[]{:S(2)}) async-start(f32[32,256,128]{2,1,0:T(8,128)} %broadcast_in_dim.26), calls=%async_computation.2 | async-start | bytes 8388608 | tf_op jit(solution)/shard_map/all_to_all | solution.py:45
  62.8 6.0 %collective-permute-start.6 = (f32[2,4,128]{2,1,0:T(4,128)S(1)}, f32[2,4,128]{2,1,0:T(4,128)S(1)}, u32[]{:S(2)}, u32[]{:S(2)}) collective-permute-start(f32[2,4,128]{2,1,0:T(4,128)S(1)} %get-tuple-element.126), channel_id=1, source_target_pairs={{2,0},{4,2},{6,4},{3,1},{5,3},{7,5},{10,8},{12,10},{14,12},{11,9},... | collective-permute-start | bytes 12296 | tf_op jit(solution)/shard_map/ppermute | solution.py:62
  67.2 5.5 %collective-permute-start.5 = (f32[2,4,128]{2,1,0:T(4,128)S(1)}, f32[2,4,128]{2,1,0:T(4,128)S(1)}, u32[]{:S(2)}, u32[]{:S(2)}) collective-permute-start(f32[2,4,128]{2,1,0:T(4,128)S(1)} %get-tuple-element.125), channel_id=1, source_target_pairs={{0,2},{2,4},{4,6},{1,3},{3,5},{5,7},{8,10},{10,12},{12,14},{9,11},... | collective-permute-start | bytes 12296 | tf_op jit(solution)/shard_map/ppermute | solution.py:59
  72.9 89.6 %collective-permute-start.8 = (f32[2,264,4]{2,1,0:T(8,128)S(1)}, f32[2,264,4]{2,1,0:T(8,128)S(1)}, u32[]{:S(2)}, u32[]{:S(2)}) collective-permute-start(f32[2,264,4]{2,1,0:T(8,128)S(1)} %get-tuple-element.108), channel_id=1, source_target_pairs={{1,0},{3,2},{5,4},{7,6},{9,8},{11,10},{13,12},{15,14},{17,16},{19,... | collective-permute-start | bytes 25352 | tf_op jit(solution)/shard_map/ppermute | solution.py:62
  74.2 88.3 %collective-permute-start.7 = (f32[2,264,4]{2,1,0:T(8,128)S(1)}, f32[2,264,4]{2,1,0:T(8,128)S(1)}, u32[]{:S(2)}, u32[]{:S(2)}) collective-permute-start(f32[2,264,4]{2,1,0:T(8,128)S(1)} %get-tuple-element.107), channel_id=1, source_target_pairs={{0,1},{2,3},{4,5},{6,7},{8,9},{10,11},{12,13},{14,15},{16,17},{18,... | collective-permute-start | bytes 25352 | tf_op jit(solution)/shard_map/ppermute | solution.py:59
  157.0 5.9 %collective-permute-start.10 = (f32[2,5,128]{2,1,0:T(8,128)S(1)}, f32[2,5,128]{2,1,0:T(8,128)S(1)}, u32[]{:S(2)}, u32[]{:S(2)}) collective-permute-start(f32[2,5,128]{2,1,0:T(8,128)S(1)} %get-tuple-element.61), channel_id=1, source_target_pairs={{2,0},{4,2},{6,4},{3,1},{5,3},{7,5},{10,8},{12,10},{14,12},{11,9},... | collective-permute-start | bytes 15368 | tf_op jit(solution)/shard_map/ppermute | solution.py:62
  161.2 5.5 %collective-permute-start.9 = (f32[2,5,128]{2,1,0:T(8,128)S(1)}, f32[2,5,128]{2,1,0:T(8,128)S(1)}, u32[]{:S(2)}, u32[]{:S(2)}) collective-permute-start(f32[2,5,128]{2,1,0:T(8,128)S(1)} %get-tuple-element.136), channel_id=1, source_target_pairs={{0,2},{2,4},{4,6},{1,3},{3,5},{5,7},{8,10},{10,12},{12,14},{9,11},... | collective-permute-start | bytes 15368 | tf_op jit(solution)/shard_map/ppermute | solution.py:59
  166.9 4.4 collective-permute-start.12
  168.2 4.2 collective-permute-start.11
  180.6 5.5 %collective-permute-start.13 = (f32[2,4,128]{2,1,0:T(4,128)S(1)}, f32[2,4,128]{2,1,0:T(4,128)S(1)}, u32[]{:S(2)}, u32[]{:S(2)}) collective-permute-start(f32[2,4,128]{2,1,0:T(4,128)S(1)} %get-tuple-element.123), channel_id=1, source_target_pairs={{0,2},{2,4},{4,6},{1,3},{3,5},{5,7},{8,10},{10,12},{12,14},{9,11},... | collective-permute-start | bytes 12296 | tf_op jit(solution)/shard_map/ppermute | solution.py:59
  186.2 4.5 %collective-permute-start.16 = (f32[2,264,4]{2,1,0:T(8,128)S(1)}, f32[2,264,4]{2,1,0:T(8,128)S(1)}, u32[]{:S(2)}, u32[]{:S(2)}) collective-permute-start(f32[2,264,4]{2,1,0:T(8,128)S(1)} %get-tuple-element.105), channel_id=1, source_target_pairs={{1,0},{3,2},{5,4},{7,6},{9,8},{11,10},{13,12},{15,14},{17,16},{19,... | collective-permute-start | bytes 25352 | tf_op jit(solution)/shard_map/ppermute | solution.py:62
  229.9 12.3 %collective-permute-start.21 = (f32[2,256,1]{2,1,0:T(8,128)S(1)}, f32[2,256,1]{2,1,0:T(8,128)S(1)}, u32[]{:S(2)}, u32[]{:S(2)}) collective-permute-start(f32[2,256,1]{2,1,0:T(8,128)S(1)} %get-tuple-element.120), channel_id=1, source_target_pairs={{1,0},{3,2},{5,4},{7,6},{9,8},{11,10},{13,12},{15,14},{17,16},{19,... | collective-permute-start | bytes 6152 | tf_op jit(solution)/shard_map/ppermute | solution.py:32
  231.2 11.0 %collective-permute-start.18 = (f32[2,256,1]{2,1,0:T(8,128)S(1)}, f32[2,256,1]{2,1,0:T(8,128)S(1)}, u32[]{:S(2)}, u32[]{:S(2)}) collective-permute-start(f32[2,256,1]{2,1,0:T(8,128)S(1)} %get-tuple-element.119), channel_id=1, source_target_pairs={{0,1},{2,3},{4,5},{6,7},{8,9},{10,11},{12,13},{14,15},{16,17},{18,... | collective-permute-start | bytes 6152 | tf_op jit(solution)/shard_map/ppermute | solution.py:31
  234.2 5.8 %collective-permute-start.20 = (f32[2,1,128]{2,1,0:T(1,128)S(1)}, f32[2,1,128]{2,1,0:T(1,128)S(1)}, u32[]{:S(2)}, u32[]{:S(2)}) collective-permute-start(f32[2,1,128]{2,1,0:T(1,128)S(1)} %get-tuple-element.118), channel_id=1, source_target_pairs={{2,0},{4,2},{6,4},{3,1},{5,3},{7,5},{10,8},{12,10},{14,12},{11,9},... | collective-permute-start | bytes 3080 | tf_op jit(solution)/shard_map/ppermute | solution.py:32
  236.7 5.5 %collective-permute-start.19 = (f32[2,1,128]{2,1,0:T(1,128)S(1)}, f32[2,1,128]{2,1,0:T(1,128)S(1)}, u32[]{:S(2)}, u32[]{:S(2)}) collective-permute-start(f32[2,1,128]{2,1,0:T(1,128)S(1)} %get-tuple-element.117), channel_id=1, source_target_pairs={{0,2},{2,4},{4,6},{1,3},{3,5},{5,7},{8,10},{10,12},{12,14},{9,11},... | collective-permute-start | bytes 3080 | tf_op jit(solution)/shard_map/ppermute | solution.py:31
  238.0 4.5 collective-permute-start.17
  279.7 96.7 %all-to-all-start.7 = ((f32[32,256,128]{2,1,0:T(8,128)}), f32[32,256,128]{2,1,0:T(8,128)}, u32[]{:S(2)}, u32[]{:S(2)}) async-start(f32[32,256,128]{2,1,0:T(8,128)} %broadcast_in_dim.29), calls=%async_computation.7 | async-start | bytes 8388608 | tf_op jit(solution)/shard_map/all_to_all | solution.py:45
  284.6 5.8 %collective-permute-start.23 = (f32[2,4,128]{2,1,0:T(4,128)S(1)}, f32[2,4,128]{2,1,0:T(4,128)S(1)}, u32[]{:S(2)}, u32[]{:S(2)}) collective-permute-start(f32[2,4,128]{2,1,0:T(4,128)S(1)} %get-tuple-element.114), channel_id=1, source_target_pairs={{2,0},{4,2},{6,4},{3,1},{5,3},{7,5},{10,8},{12,10},{14,12},{11,9},... | collective-permute-start | bytes 12296 | tf_op jit(solution)/shard_map/ppermute | solution.py:62
  289.1 5.5 %collective-permute-start.22 = (f32[2,4,128]{2,1,0:T(4,128)S(1)}, f32[2,4,128]{2,1,0:T(4,128)S(1)}, u32[]{:S(2)}, u32[]{:S(2)}) collective-permute-start(f32[2,4,128]{2,1,0:T(4,128)S(1)} %get-tuple-element.113), channel_id=1, source_target_pairs={{0,2},{2,4},{4,6},{1,3},{3,5},{5,7},{8,10},{10,12},{12,14},{9,11},... | collective-permute-start | bytes 12296 | tf_op jit(solution)/shard_map/ppermute | solution.py:59
  294.8 89.6 %collective-permute-start.25 = (f32[2,264,4]{2,1,0:T(8,128)S(1)}, f32[2,264,4]{2,1,0:T(8,128)S(1)}, u32[]{:S(2)}, u32[]{:S(2)}) collective-permute-start(f32[2,264,4]{2,1,0:T(8,128)S(1)} %get-tuple-element.100), channel_id=1, source_target_pairs={{1,0},{3,2},{5,4},{7,6},{9,8},{11,10},{13,12},{15,14},{17,16},{19,... | collective-permute-start | bytes 25352 | tf_op jit(solution)/shard_map/ppermute | solution.py:62
  296.1 88.3 %collective-permute-start.24 = (f32[2,264,4]{2,1,0:T(8,128)S(1)}, f32[2,264,4]{2,1,0:T(8,128)S(1)}, u32[]{:S(2)}, u32[]{:S(2)}) collective-permute-start(f32[2,264,4]{2,1,0:T(8,128)S(1)} %get-tuple-element.99), channel_id=1, source_target_pairs={{0,1},{2,3},{4,5},{6,7},{8,9},{10,11},{12,13},{14,15},{16,17},{18,... | collective-permute-start | bytes 25352 | tf_op jit(solution)/shard_map/ppermute | solution.py:59
  378.9 5.8 %collective-permute-start.27 = (f32[2,5,128]{2,1,0:T(8,128)S(1)}, f32[2,5,128]{2,1,0:T(8,128)S(1)}, u32[]{:S(2)}, u32[]{:S(2)}) collective-permute-start(f32[2,5,128]{2,1,0:T(8,128)S(1)} %get-tuple-element.134), channel_id=1, source_target_pairs={{2,0},{4,2},{6,4},{3,1},{5,3},{7,5},{10,8},{12,10},{14,12},{11,9},... | collective-permute-start | bytes 15368 | tf_op jit(solution)/shard_map/ppermute | solution.py:62
  383.1 5.5 %collective-permute-start.26 = (f32[2,5,128]{2,1,0:T(8,128)S(1)}, f32[2,5,128]{2,1,0:T(8,128)S(1)}, u32[]{:S(2)}, u32[]{:S(2)}) collective-permute-start(f32[2,5,128]{2,1,0:T(8,128)S(1)} %get-tuple-element.133), channel_id=1, source_target_pairs={{0,2},{2,4},{4,6},{1,3},{3,5},{5,7},{8,10},{10,12},{12,14},{9,11},... | collective-permute-start | bytes 15368 | tf_op jit(solution)/shard_map/ppermute | solution.py:59
  388.8 4.6 %collective-permute-start.29 = (f32[2,266,5]{2,1,0:T(8,128)S(1)}, f32[2,266,5]{2,1,0:T(8,128)S(1)}, u32[]{:S(2)}, u32[]{:S(2)}) collective-permute-start(f32[2,266,5]{2,1,0:T(8,128)S(1)} %get-tuple-element.90), channel_id=1, source_target_pairs={{1,0},{3,2},{5,4},{7,6},{9,8},{11,10},{13,12},{15,14},{17,16},{19,... | collective-permute-start | bytes 31928 | tf_op jit(solution)/shard_map/ppermute | solution.py:62
  390.1 4.2 collective-permute-start.28
  402.2 5.5 %collective-permute-start.30 = (f32[2,4,128]{2,1,0:T(4,128)S(1)}, f32[2,4,128]{2,1,0:T(4,128)S(1)}, u32[]{:S(2)}, u32[]{:S(2)}) collective-permute-start(f32[2,4,128]{2,1,0:T(4,128)S(1)} %get-tuple-element.111), channel_id=1, source_target_pairs={{0,2},{2,4},{4,6},{1,3},{3,5},{5,7},{8,10},{10,12},{12,14},{9,11},... | collective-permute-start | bytes 12296 | tf_op jit(solution)/shard_map/ppermute | solution.py:59
  407.9 4.4 collective-permute-start.33
  (10 other events, 150.0 us)
where the time goes:
time: 453 us; the launch traced here: 452 us
  waiting for transfers between devices  188 us (42%)
  blocking collectives  136 us (30%)
  starting transfers between devices  88 us (19%)
  other arithmetic  28.4 us (6%)
  local copies, waits for them, and re-layouts  7.48 us (2%)
    all_to_all x2, waiting for transfers between devices, from_everyone(): lax.all_to_all(jnp.broadcast_to(array[None], (peers, *array.shape)), axis...  155 us
    all_to_all x2, blocking collectives, body(): lax.all_to_all(source[None], 'tm', split_axis=1, concat_axis=0, tiled=True)  42 us
    all_to_all x2, blocking collectives, body(): lax.all_to_all(jnp.stack([solution_real, solution_imag])[:, None], 'tm',...  36.8 us
    ppermute x12, starting transfers between devices, extended(): lax.ppermute(lax.slice_in_dim(block, 0, width, axis=dim), axis, backward)  29.8 us
    all_to_all x2, blocking collectives, forward_block(): lax.all_to_all(jnp.stack([real_part, imag_part]), 'tm', split_axis=1, con...  29.5 us
    ppermute x12, waiting for transfers between devices, extended(): lax.ppermute(lax.slice_in_dim(block, block.shape[dim] - width, None, axis...  28.5 us
    all_to_all x2, blocking collectives, inverse_block(): return lax.all_to_all(values, 'tm', split_axis=0, concat_axis=1, tiled=True)  28.2 us
    ppermute x12, starting transfers between devices, extended(): lax.ppermute(lax.slice_in_dim(block, block.shape[dim] - width, None, axis...  26.5 us
  transfers between devices with their start and end apart: 36, of which 15 were waited for; matrix products, arithmetic and copies ran while one was open for 1% of the time, Pallas kernels for 0%

commit v1 on v0

v1 whole, which is shorter than its diff:
```python
import functools
import math

import jax
import jax.numpy as jnp
from jax import lax
from jax.experimental import pallas as pl
from jax.experimental.pallas import tpu as pltpu
from jax.sharding import PartitionSpec as P

NEWTON = 2
SWEEPS = 8
RING_Y = 4
ROWS = 8
LANES = 128
WIDE = 2 * LANES
EXT = 3 * ROWS

circulant_weight = 0.25
time_step = 1.0
MESH = pl.DeviceIdType.MESH


def forward_modes(u, half, levels, odd):
    mid = half // 2
    out = []
    if not odd:
        even = [u[l] + u[half - l] for l in range(1, mid)]
        diff = [u[l] - u[half - l] for l in range(1, mid)]
        plus, minus = u[0] + u[mid], u[0] - u[mid]
        for m in range(mid):
            real = plus if m % 2 == 0 else minus
            for l in range(1, mid):
                real = real + even[l - 1] * math.cos(2 * math.pi * l * m / half)
            if m == 0:
                imag = plus if mid % 2 == 0 else minus
                for l in range(1, mid):
                    imag = imag + even[l - 1] * (-1.0) ** l
            else:
                imag = None
                for l in range(1, mid):
                    term = diff[l - 1] * -math.sin(2 * math.pi * l * m / half)
                    imag = term if imag is None else imag + term
            out.append((real, imag))
    else:
        diff = [u[l] - u[half - l] for l in range(1, mid)]
        both = [u[l] + u[half - l] for l in range(1, mid)]
        for m in range(mid):
            k = 2 * m + 1
            real = u[0]
            imag = u[mid] * -math.sin(math.pi * k / 2)
            for l in range(1, mid):
                real = real + diff[l - 1] * math.cos(2 * math.pi * l * k / levels)
                imag = imag + both[l - 1] * -math.sin(2 * math.pi * l * k / levels)
            out.append((real, imag))
    return out


def inverse_modes(v, half, levels, odd):
    mid = half // 2
    out = [None] * half
    scale = 2.0 / levels
    for l in range(mid + 1):
        if not odd:
            cosine = v[0] * (1.0 / levels) + v[1] * ((-1.0) ** l / levels)
            sine = None
            for m in range(1, mid):
                cosine = cosine + v[2 * m] * (scale * math.cos(2 * math.pi * l * m / half))
                if l not in (0, mid):
                    term = v[2 * m + 1] * (scale * math.sin(2 * math.pi * l * m / half))
                    sine = term if sine is None else sine + term
            low = cosine if sine is None else cosine - sine
            high = cosine if sine is None else cosine + sine
        else:
            cosine = sine = None
            for m in range(mid):
                k = 2 * m + 1
                term = v[2 * m] * (scale * math.cos(2 * math.pi * l * k / levels))
                cosine = term if cosine is None else cosine + term
                if l > 0:
                    term = v[2 * m + 1] * (scale * math.sin(2 * math.pi * l * k / levels))
                    sine = term if sine is None else sine + term
            low = cosine if sine is None else cosine - sine
            high = -cosine if sine is None else -cosine - sine
        out[l] = low
        if 0 < l < half:
            out[half - l] = high if l != mid else low
    return out


def kernel(
    levels, stripes,
    guess_ref, start_ref, bed_ref, rate_ref, balance_ref, flags_ref,
    out_ref,
    guess, balance, bed_in, rate_in, flags_in,
    own, edge, mass, stat_send, stat, row_send, rows,
    dsend, dext, resid, ysend, yext, coef, weight, modes, parts, dummy,
    load_sem, gsend, grecv, bsend, brecv, ssend, srecv, osend, orecv,
    esend, erecv, hsend, hrecv, dsem_s, dsem_r, ysem_s, ysem_r, psem_s, psem_r,
):
    half = levels // 2
    slots = half // 2
    ring_z = levels // RING_Y
    tiles = stripes * levels
    root = circulant_weight ** (1.0 / levels)

    level = lax.axis_index("tm")
    sx = lax.axis_index("sx")
    core = lax.axis_index("sy")
    other = 1 - core
    mine = pl.ds(pl.multiple_of(core * LANES, LANES), LANES)
    theirs = pl.ds(pl.multiple_of(other * LANES, LANES), LANES)

    def tile_of(stripe, tm):
        z, y = tm // RING_Y, tm % RING_Y
        place = z * RING_Y + jnp.where(z % 2 == 0, y, RING_Y - 1 - y)
        return jnp.where(stripe % 2 == 0, place, levels - 1 - place)

    def owner_of(stripe, tile):
        place = jnp.where(stripe % 2 == 0, tile, levels - 1 - tile)
        z, y = place // RING_Y, place % RING_Y
        return z * RING_Y + jnp.where(z % 2 == 0, y, RING_Y - 1 - y)

    tile = tile_of(sx, level)
    strip = sx * levels + tile
    above = (strip + tiles - 1) % tiles
    below = (strip + 1) % tiles
    above_sx, below_sx = above // levels, below // levels
    above_tm = owner_of(above_sx, above % levels)
    below_tm = owner_of(below_sx, below % levels)
    has_above = strip > 0
    has_below = strip < tiles - 1

    def peer(step):
        iz, iy = step // RING_Y, step % RING_Y
        sign_z = 1 - 2 * (iz % 2)
        sign_y = 1 - 2 * (iy % 2)
        z = (level // RING_Y + ring_z // 2 + sign_z * ((iz + 1) // 2) + ring_z) % ring_z
        y = (level % RING_Y + RING_Y // 2 + sign_y * ((iy + 1) // 2) + RING_Y) % RING_Y
        return z * RING_Y + y

    def send(src, dst, ssem, rsem, device):
        pltpu.make_async_remote_copy(
            src_ref=src, dst_ref=dst, send_sem=ssem, recv_sem=rsem,
            device_id=device, device_id_type=MESH,
        ).start()

    def wait(sem, count):
        view = dummy.at[pl.ds(0, count)]
        pltpu.make_async_copy(view, view, sem).wait()

    def around(src, place, ssem, rsem):
        send(src, place(1), ssem, rsem, (level, sx, other))
        for to in range(2):
            send(src, place(2), ssem, rsem, (above_tm, above_sx, to))
            send(src, place(0), ssem, rsem, (below_tm, below_sx, to))

    barrier = pltpu.get_barrier_semaphore()

    def greet(step, carry):
        pl.semaphore_signal(barrier, inc=1, device_id=(peer(step), sx, core), device_id_type=MESH)
        return carry

    lax.fori_loop(0, levels - 1, greet, 0)
    pl.semaphore_signal(barrier, inc=1, device_id=(level, sx, other), device_id_type=MESH)
    for to in range(2):
        pl.semaphore_signal(barrier, inc=1, device_id=(above_tm, above_sx, to), device_id_type=MESH)
        pl.semaphore_signal(barrier, inc=1, device_id=(below_tm, below_sx, to), device_id_type=MESH)

    here = pl.ds(pl.multiple_of(tile * ROWS, ROWS), ROWS)
    loads = [
        pltpu.make_async_copy(guess_ref.at[0], guess, load_sem.at[0]),
        pltpu.make_async_copy(balance_ref.at[0], balance, load_sem.at[1]),
        pltpu.make_async_copy(bed_ref.at[here], bed_in, load_sem.at[2]),
        pltpu.make_async_copy(rate_ref.at[here], rate_in, load_sem.at[3]),
        pltpu.make_async_copy(flags_ref.at[here], flags_in, load_sem.at[4]),
        pltpu.make_async_copy(start_ref.at[here], own.at[0, :, mine], load_sem.at[5]),
    ]
    for load in loads:
        load.start()
    for load in loads:
        load.wait()

    inside_own = (flags_in[...] != 0).astype(jnp.float32)
    boost = 1.0 + (flags_in[...] == 2).astype(jnp.float32)
    cst_own = inside_own * boost * rate_in[...]
    bed_own = bed_in[...]
    for i, value in enumerate((cst_own, bed_own, inside_own)):
        stat_send[i] = value
        stat[i, ROWS : 2 * ROWS, mine] = value

    pl.semaphore_wait(barrier, levels - 1 + 5)

    def scatter(src, dst, ssem, rsem):
        def step(i, carry):
            to = peer(i)
            rows_to = pl.ds(pl.multiple_of(tile_of(sx, to) * ROWS, ROWS), ROWS)
            send(src.at[rows_to], dst, ssem, rsem, (to, sx, core))
            return carry

        lax.fori_loop(0, levels - 1, step, 0)

    scatter(guess, own.at[1 + level, :, mine], gsend, grecv)
    scatter(balance, mass.at[level], bsend, brecv)
    around(
        stat_send, lambda p: stat.at[:, pl.ds(p * ROWS, ROWS), mine], ssend, srecv
    )
    own[1 + level, :, mine] = guess[here]
    mass[level] = balance[here]

    wait(grecv, levels - 1)
    all_levels = pl.ds(1, levels)
    send(
        own.at[all_levels, :, mine], own.at[all_levels, :, mine], hsend, hrecv,
        (level, sx, other),
    )
    for l in range(levels):
        row_send[0, l : l + 1] = own[1 + l, 0:1, mine]
        row_send[1, l : l + 1] = own[1 + l, ROWS - 1 : ROWS, mine]
    send(row_send.at[0], rows.at[1], esend, erecv, (above_tm, above_sx, core))
    send(row_send.at[1], rows.at[0], esend, erecv, (below_tm, below_sx, core))

    row8 = lax.broadcasted_iota(jnp.int32, (ROWS, LANES), 0)
    lane = lax.broadcasted_iota(jnp.int32, (ROWS, LANES), 1)
    first_row, last_row = row8 == 0, row8 == ROWS - 1
    first_lane, last_lane = lane == 0, lane == LANES - 1
    edge_valid = (last_row & has_above) | (first_row & has_below)

    def neighbours(x, x_other, x_edge):
        right = pltpu.roll(jnp.where(first_lane, jnp.where(core == 0, x_other, 0.0), x), LANES - 1, 1)
        left = pltpu.roll(jnp.where(last_lane, jnp.where(core == 1, x_other, 0.0), x), 1, 1)
        down = pltpu.roll(jnp.where(first_row, x_edge, x), ROWS - 1, 0)
        up = pltpu.roll(jnp.where(last_row, x_edge, x), 1, 0)
        return right, left, down, up

    wait(srecv, 3 * 5)
    wait(erecv, 2 * (levels // ROWS))
    for l in range(levels):
        edge[l] = jnp.where(last_row, rows[0, l : l + 1], rows[1, l : l + 1])

    cst_other = stat[0, ROWS : 2 * ROWS, theirs]
    bed_other = stat[1, ROWS : 2 * ROWS, theirs]
    cst_edge = jnp.where(
        edge_valid, jnp.where(last_row, stat[0, 0:ROWS, mine], stat[0, 2 * ROWS :, mine]), 0.0
    )
    bed_edge = jnp.where(last_row, stat[1, 0:ROWS, mine], stat[1, 2 * ROWS :, mine])

    row_wide = lax.broadcasted_iota(jnp.int32, (EXT, WIDE), 0)
    col_wide = lax.broadcasted_iota(jnp.int32, (EXT, WIDE), 1)
    valid_wide = (
        ((row_wide >= ROWS) | has_above) & ((row_wide < 2 * ROWS) | has_below)
    )

    wait(hrecv, levels)

    def diffusivity(scale, h):
        return scale * h * h * jnp.abs(h)

    def newton(n, carry):
        def add_up(l, sums):
            return (
                sums[0] + diffusivity(cst_own, own[1 + l, :, mine]),
                sums[1] + diffusivity(cst_other, own[1 + l, :, theirs]),
                sums[2] + diffusivity(cst_edge, edge[l]),
            )

        zero = jnp.zeros((ROWS, LANES), jnp.float32)
        sums = lax.fori_loop(0, levels, add_up, (zero, zero, zero))
        mean, mean_other, mean_edge = (s * (1.0 / levels) for s in sums)
        total = 0.5 * (4.0 * mean + sum(neighbours(mean, mean_other, mean_edge)))
        for i, value in enumerate((mean, total)):
            dsend[n, i] = value
            dext[n, i, ROWS : 2 * ROWS, mine] = value
        around(
            dsend.at[n],
            lambda p: dext.at[n, :, pl.ds(p * ROWS, ROWS), mine],
            dsem_s.at[n], dsem_r.at[n],
        )

        @pl.when(n == 0)
        def _():
            wait(brecv, levels - 1)

        def residual(l, lift):
            h, h_other, h_edge = own[1 + l, :, mine], own[1 + l, :, theirs], edge[l]
            d = diffusivity(cst_own, h)
            s = h + bed_own
            d_near = neighbours(
                d, diffusivity(cst_other, h_other), diffusivity(cst_edge, h_edge)
            )
            s_near = neighbours(
                s, h_other + bed_other, jnp.where(edge_valid, h_edge + bed_edge, 0.0)
            )
            flux = sum((d + dn) * (s - sn) for dn, sn in zip(d_near, s_near))
            change = (h - own[l, :, mine]) / time_step + 0.5 * flux - mass[l]
            resid[l] = inside_own * change * lift
            return lift * root

        lax.fori_loop(0, levels, residual, jnp.ones((ROWS, LANES), jnp.float32))

        low = [resid[l] for l in range(half)]
        high = [resid[l + half] for l in range(half)]
        evens = forward_modes([a + b for a, b in zip(low, high)], half, levels, False)
        odds = forward_modes([a - b for a, b in zip(low, high)], half, levels, True)
        for slot in range(slots):
            for i in range(2):
                ysend[n, 0, 2 * slot + i] = evens[slot][i]
                ysend[n, 1, 2 * slot + i] = odds[slot][i]
                yext[n, 2 * slot + i, ROWS : 2 * ROWS, mine] = jnp.where(
                    core == 0, evens[slot][i], odds[slot][i]
                )
            pair = pl.ds(2 * slot, 2)

            def place(p):
                return yext.at[n, pair, pl.ds(p * ROWS, ROWS), mine]

            s_sem, r_sem = ysem_s.at[n], ysem_r.at[n, slot]
            send(ysend.at[n, other, pair], place(1), s_sem, r_sem, (level, sx, other))
            for to in range(2):
                send(ysend.at[n, to, pair], place(2), s_sem, r_sem, (above_tm, above_sx, to))
                send(ysend.at[n, to, pair], place(0), s_sem, r_sem, (below_tm, below_sx, to))

        wait(dsem_r.at[n], 2 * 5)
        mean_wide = jnp.where(valid_wide, dext[n, 0], 0.0)
        total_wide = dext[n, 1]
        inside_wide = jnp.where(valid_wide, stat[2], 0.0)
        weight[0] = jnp.where(
            col_wide == WIDE - 1, 0.0, 0.5 * (mean_wide + pltpu.roll(mean_wide, WIDE - 1, 1))
        )
        weight[1] = jnp.where(col_wide == 0, 0.0, 0.5 * (mean_wide + pltpu.roll(mean_wide, 1, 1)))
        weight[2] = 0.5 * (mean_wide + pltpu.roll(mean_wide, EXT - 1, 0))
        weight[3] = 0.5 * (mean_wide + pltpu.roll(mean_wide, 1, 0))
        for m in range(slots):
            def shift(k):
                angle = 2 * math.pi * k / levels
                return (
                    (1.0 - root * math.cos(angle)) / time_step,
                    root * math.sin(angle) / time_step,
                )

            even_real, even_imag = shift(2 * m)
            odd_real, odd_imag = shift(2 * m + 1)
            last_real = shift(half)[0] if m == 0 else even_real
            real = total_wide + jnp.where(core == 0, even_real, odd_real)
            real_2 = total_wide + jnp.where(core == 0, last_real, odd_real)
            imag = jnp.where(core == 0, 0.0 if m == 0 else even_imag, odd_imag)
            scaled = inside_wide / (real * real + imag * imag)
            coef[m, 0] = scaled * real
            coef[m, 1] = scaled * -imag
            coef[m, 2] = inside_wide * real_2 / (real_2 * real_2 + imag * imag)

        def solve(slot, carry):
            wait(ysem_r.at[n, slot], 2 * 5)
            source_real = yext[n, 2 * slot]
            source_imag = yext[n, 2 * slot + 1]
            a, b, c = coef[slot, 0], coef[slot, 1], coef[slot, 2]

            def apply(real, imag):
                return real * a - imag * b, real * b + imag * c

            def spread(v):
                return (
                    weight[0] * pltpu.roll(v, WIDE - 1, 1)
                    + weight[1] * pltpu.roll(v, 1, 1)
                    + weight[2] * pltpu.roll(v, EXT - 1, 0)
                    + weight[3] * pltpu.roll(v, 1, 0)
                )

            real, imag = apply(source_real, source_imag)
            for _ in range(SWEEPS - 1):
                real, imag = apply(source_real + spread(real), source_imag + spread(imag))
            for i, v in enumerate((real, imag)):
                for h in range(2):
                    cols = slice(h * LANES, (h + 1) * LANES)
                    modes[h, 2 * slot + i] = v[ROWS : 2 * ROWS, cols]
                    modes[2 + h, 2 * slot + i] = jnp.where(last_row, v[0:ROWS, cols], v[2 * ROWS :, cols])
            return carry

        lax.fori_loop(0, slots, solve, 0)

        for parity in range(2):
            @pl.when(core == parity)
            def _():
                def invert(p, carry):
                    values = inverse_modes(
                        [modes[p, f] for f in range(half)], half, levels, parity == 1
                    )
                    for l in range(half):
                        parts[n, parity, p, l] = values[l]
                    return carry

                lax.fori_loop(0, 4, invert, 0)

        send(
            parts.at[n, core], parts.at[n, core], psem_s.at[n], psem_r.at[n], (level, sx, other)
        )
        wait(psem_r.at[n], 4 * half)

        def update(l, drop):
            far = drop * (root ** -half)
            for h in range(2):
                cols = slice(h * LANES, (h + 1) * LANES)
                p, q = parts[n, 0, h, l], parts[n, 1, h, l]
                own[1 + l, :, cols] = own[1 + l, :, cols] - (p + q) * drop
                own[1 + half + l, :, cols] = own[1 + half + l, :, cols] - (p - q) * far
            p, q = parts[n, 0, 2 + core, l], parts[n, 1, 2 + core, l]
            edge[l] = edge[l] - (p + q) * drop
            edge[half + l] = edge[half + l] - (p - q) * far
            return drop * (1.0 / root)

        @pl.when(n == 0)
        def _():
            wait(hsend, levels)

        lax.fori_loop(0, half, update, jnp.ones((ROWS, LANES), jnp.float32))
        return carry

    lax.fori_loop(0, NEWTON, newton, 0)

    def give(i, carry):
        to = peer(i)
        send(own.at[1 + to, :, mine], out_ref.at[0, here], osend, orecv, (to, sx, core))
        return carry

    lax.fori_loop(0, levels - 1, give, 0)
    out_ref[0, here] = own[1 + level, :, mine]

    wait(gsend, levels - 1)
    wait(bsend, levels - 1)
    wait(ssend, 3 * 5)
    wait(esend, 2 * (levels // ROWS))
    for n in range(NEWTON):
        wait(dsem_s.at[n], 2 * 5)
        wait(ysem_s.at[n], 2 * 5 * slots)
        wait(psem_s.at[n], 4 * half)
    wait(osend, levels - 1)
    wait(orecv, levels - 1)


def solution(mesh):
    levels, stripes = mesh.shape["tm"], mesh.shape["sx"]
    half = levels // 2
    slots = half // 2
    tile = (ROWS, LANES)
    f32 = jnp.float32

    def vmem(*lead, last=tile, dtype=f32):
        return pltpu.VMEM((*lead, *last), dtype)

    dma = pltpu.SemaphoreType.DMA

    def body(guess, start, bed, rate, balance, flags):
        rows = guess.shape[1]
        return pl.pallas_call(
            functools.partial(kernel, levels, stripes),
            out_shape=jax.ShapeDtypeStruct(guess.shape, f32),
            in_specs=[pl.BlockSpec(memory_space=pl.ANY)] * 6,
            out_specs=pl.BlockSpec(memory_space=pltpu.VMEM),
            scratch_shapes=[
                vmem(last=(rows, LANES)), vmem(last=(rows, LANES)),
                vmem(), vmem(), vmem(dtype=jnp.int32),
                vmem(levels + 1, last=(ROWS, WIDE)), vmem(levels), vmem(levels),
                vmem(3), vmem(3, last=(EXT, WIDE)),
                vmem(2, last=(levels, LANES)), vmem(2, last=(levels, LANES)),
                vmem(NEWTON, 2), vmem(NEWTON, 2, last=(EXT, WIDE)),
                vmem(levels), vmem(NEWTON, 2, half),
                vmem(NEWTON, half, last=(EXT, WIDE)),
                vmem(slots, 3, last=(EXT, WIDE)), vmem(4, last=(EXT, WIDE)),
                vmem(4, half), vmem(NEWTON, 2, 4, half),
                vmem(max(2 * 5 * slots, 4 * half, levels)),
                dma((6,)), dma, dma, dma, dma, dma, dma, dma, dma,
                dma, dma, dma, dma, dma((NEWTON,)), dma((NEWTON,)),
                dma((NEWTON,)), dma((NEWTON, slots)), dma((NEWTON,)), dma((NEWTON,)),
            ],
            compiler_params=pltpu.CompilerParams(collective_id=0, has_side_effects=True),
        )(guess, start, bed, rate, balance, flags)

    return jax.shard_map(
        body, mesh=mesh,
        in_specs=(
            P("tm", "sx", "sy"), P("sx", "sy"), P("sx", "sy"), P("sx", "sy"),
            P("tm", "sx", "sy"), P("sx", "sy"),
        ),
        out_specs=P("tm", "sx", "sy"), check_vma=False,
    )
```

time: 453 us -> 55.3 us (0.12)
  waiting for transfers between devices: 188 us -> 0 us
  blocking collectives: 136 us -> 0 us
  starting transfers between devices: 88 us -> 0 us
  Pallas kernels: 0 us -> 53.6 us
  other arithmetic: 28.4 us -> 0 us
  local copies, waits for them, and re-layouts: 7.48 us -> 1.57 us
    all_to_all x2 -> x0, waiting for transfers between devices: 155 us -> none  [from_everyone(): lax.all_to_all(jnp.broadcast_to(array[None], (peers, *array.shape)), axis...]
    all_to_all x8 -> x0, blocking collectives: 136 us -> none  [the longest x2 42 us: body(): lax.all_to_all(source[None], 'tm', split_axis=1, concat_axis=0, tiled=True)]
    ppermute x34 -> x0, starting transfers between devices: 78.3 us -> none  [the longest x12 29.8 us: extended(): lax.ppermute(lax.slice_in_dim(block, 0, width, axis=dim), axis, backward)]
    pallas_call x0 -> x1, Pallas kernels: none -> 53.6 us  [body(): pl.pallas_call(functools.partial(kernel, levels, stripes), out_shape=jax....]
    ppermute x34 -> x0, waiting for transfers between devices: 33.1 us -> none  [the longest x12 28.5 us: extended(): lax.ppermute(lax.slice_in_dim(block, block.shape[dim] - width, None, axis...]
    add x25 -> x0, other arithmetic: 14.9 us -> none  [the longest x8 8.64 us: jacobi_sweeps(): value_real = numer_real * local_coeffs[0] + numer_imag * local_coeffs[1]]
    all_to_all x2 -> x0, starting transfers between devices: 9.71 us -> none  [from_everyone(): lax.all_to_all(jnp.broadcast_to(array[None], (peers, *array.shape)), axis...]
    broadcast_in_dim x4 -> x0, local copies, waits for them, and re-layouts: 5.44 us -> none  [the longest x2 5.03 us: from_everyone(): jnp.broadcast_to(array[None], (peers, *array.shape))]
  transfers between devices with their start and end apart: 36 -> 0, of which waited for: 15 -> 0; matrix products, arithmetic and copies ran while one was open for 1% -> 0% of each run, Pallas kernels for 0% -> 0%
where the time goes in v1:
time: 55.3 us; the launch traced here: 55.2 us
  Pallas kernels  53.6 us (97%)
  local copies, waits for them, and re-layouts  1.57 us (3%)
    pallas_call x1, Pallas kernels, body(): pl.pallas_call(functools.partial(kernel, levels, stripes), out_shape=jax....  53.6 us
    unnamed x1, local copies, waits for them, and re-layouts  1.57 us

profile of v1, /device:TPU:6, one launch (start us, length us, event | category | flops | bytes accessed | tf_op | source)
XLA Modules:
  0.0 55.2 jit_solution(6188409172735697194)
XLA Ops:
  0.0 53.6 %shard_map.64 = f32[1,256,128]{2,1,0:T(8,128)} custom-call(f32[1,256,128]{2,1,0:T(8,128)} %guess_ref.1, f32[256,128]{1,0:T(8,128)} %start_ref.1, f32[256,128]{1,0:T(8,128)} %bed_ref.1, f32[256,128]{1,0:T(8,128)} %rate_ref.1, f32[1,256,128]{2,1,0:T(8,128)} %balance_ref.1, s32[256,128]{1,0:T(8,128)} %flags_ref.1), custom_call_target="tpu_custom_call" | custom-call | tf_op jit(solution)/shard_map/pallas_call | solution.py:454
  53.6 1.6 %copy.8 = f32[1,256,128]{2,1,0:T(8,128)} copy(f32[1,256,128]{2,1,0:T(8,128)} %shard_map.64) | data formatting | bytes 262144

commit v2 on v1

v2 whole, which is shorter than its diff:
```python
import functools
import math

import jax
import jax.numpy as jnp
from jax import lax
from jax.experimental import pallas as pl
from jax.experimental.pallas import tpu as pltpu
from jax.sharding import PartitionSpec as P

NEWTON = 2
SWEEPS = 8
RING_Y = 4
ROWS = 8
LANES = 128
EXT = 3 * ROWS
GROUP = 4

circulant_weight = 0.25
time_step = 1.0
MESH = pl.DeviceIdType.MESH


def forward_modes(u, half, levels, odd):
    mid = half // 2
    out = []
    if not odd:
        even = [u[l] + u[half - l] for l in range(1, mid)]
        diff = [u[l] - u[half - l] for l in range(1, mid)]
        plus, minus = u[0] + u[mid], u[0] - u[mid]
        for m in range(mid):
            real = plus if m % 2 == 0 else minus
            for l in range(1, mid):
                real = real + even[l - 1] * math.cos(2 * math.pi * l * m / half)
            if m == 0:
                imag = plus if mid % 2 == 0 else minus
                for l in range(1, mid):
                    imag = imag + even[l - 1] * (-1.0) ** l
            else:
                imag = None
                for l in range(1, mid):
                    term = diff[l - 1] * -math.sin(2 * math.pi * l * m / half)
                    imag = term if imag is None else imag + term
            out.append((real, imag))
    else:
        diff = [u[l] - u[half - l] for l in range(1, mid)]
        both = [u[l] + u[half - l] for l in range(1, mid)]
        for m in range(mid):
            k = 2 * m + 1
            real = u[0]
            imag = u[mid] * -math.sin(math.pi * k / 2)
            for l in range(1, mid):
                real = real + diff[l - 1] * math.cos(2 * math.pi * l * k / levels)
                imag = imag + both[l - 1] * -math.sin(2 * math.pi * l * k / levels)
            out.append((real, imag))
    return out


def inverse_modes(v, half, levels, odd):
    mid = half // 2
    out = [None] * half
    scale = 2.0 / levels
    for l in range(mid + 1):
        if not odd:
            cosine = v[0] * (1.0 / levels) + v[1] * ((-1.0) ** l / levels)
            sine = None
            for m in range(1, mid):
                cosine = cosine + v[2 * m] * (scale * math.cos(2 * math.pi * l * m / half))
                if l not in (0, mid):
                    term = v[2 * m + 1] * (scale * math.sin(2 * math.pi * l * m / half))
                    sine = term if sine is None else sine + term
            low = cosine if sine is None else cosine - sine
            high = cosine if sine is None else cosine + sine
        else:
            cosine = sine = None
            for m in range(mid):
                k = 2 * m + 1
                term = v[2 * m] * (scale * math.cos(2 * math.pi * l * k / levels))
                cosine = term if cosine is None else cosine + term
                if l > 0:
                    term = v[2 * m + 1] * (scale * math.sin(2 * math.pi * l * k / levels))
                    sine = term if sine is None else sine + term
            low = cosine if sine is None else cosine - sine
            high = -cosine if sine is None else -cosine - sine
        out[l] = low
        if 0 < l < half:
            out[half - l] = high if l != mid else low
    return out


def kernel(
    levels, stripes,
    guess_ref, start_ref, bed_ref, rate_ref, balance_ref, flags_ref,
    out_ref,
    guess, balance, bed_in, rate_in, flags_in,
    own, edge, mass, stat_send, stat, row_send, rows,
    dsend, dext, resid, ysend, yext, coef, mean_pad, weight, work, modes, parts, dummy,
    load_sem, gsend, grecv, bsend, brecv, ssend, srecv, osend, orecv,
    esend, erecv, hsend, hrecv, dsem_s, dsem_r, ysem_s, ysem_r,
    psem_s, psem_r, qsem_s, qsem_r,
):
    half = levels // 2
    slots = half // 2
    ring_z = levels // RING_Y
    tiles = stripes * levels
    root = circulant_weight ** (1.0 / levels)
    group = min(GROUP, slots)

    level = lax.axis_index("tm")
    sx = lax.axis_index("sx")
    core = lax.axis_index("sy")
    other = 1 - core

    def turned(stripe, index):
        return index ^ ((stripe & 1) * (levels - 1))

    def snake(index):
        return index ^ (((index >> 2) & 1) * (RING_Y - 1))

    def tile_of(stripe, tm):
        return turned(stripe, snake(tm))

    def owner_of(stripe, tile):
        return snake(turned(stripe, tile))

    tile = tile_of(sx, level)
    strip = sx * levels + tile
    above = (strip + tiles - 1) & (tiles - 1)
    below = (strip + 1) & (tiles - 1)
    above_sx, below_sx = lax.div(above, levels), lax.div(below, levels)
    above_tm = owner_of(above_sx, above & (levels - 1))
    below_tm = owner_of(below_sx, below & (levels - 1))
    has_above = strip > 0
    has_below = strip < tiles - 1

    def reach(code, ring):
        return -sum(min((p ^ code) - p & ring - 1, p - (p ^ code) & ring - 1) for p in range(ring))

    far_z = sorted(range(ring_z), key=lambda code: reach(code, ring_z))
    far_y = sorted(range(RING_Y), key=lambda code: reach(code, RING_Y))
    peers = [level ^ (z * RING_Y + y) for z in far_z for y in far_y if z or y]

    def send(src, dst, ssem, rsem, device):
        pltpu.make_async_remote_copy(
            src_ref=src, dst_ref=dst, send_sem=ssem, recv_sem=rsem,
            device_id=device, device_id_type=MESH,
        ).start()

    def wait(sem, count):
        view = dummy.at[pl.ds(0, count)]
        pltpu.make_async_copy(view, view, sem).wait()

    def around(src, place, ssem, rsem):
        for to in range(2):
            send(src, place(2), ssem, rsem, (above_tm, above_sx, to))
            send(src, place(0), ssem, rsem, (below_tm, below_sx, to))
        send(src, place(1), ssem, rsem, (level, sx, other))

    barrier = pltpu.get_barrier_semaphore()

    def greet(device):
        pl.semaphore_signal(barrier, inc=1, device_id=device, device_id_type=MESH)

    for peer in peers:
        greet((peer, sx, core))
    greet((level, sx, other))
    for to in range(2):
        greet((above_tm, above_sx, to))
        greet((below_tm, below_sx, to))

    here = pl.ds(pl.multiple_of(tile * ROWS, ROWS), ROWS)
    loads = [
        pltpu.make_async_copy(guess_ref.at[0], guess, load_sem.at[0]),
        pltpu.make_async_copy(balance_ref.at[0], balance, load_sem.at[1]),
        pltpu.make_async_copy(bed_ref.at[here], bed_in, load_sem.at[2]),
        pltpu.make_async_copy(rate_ref.at[here], rate_in, load_sem.at[3]),
        pltpu.make_async_copy(flags_ref.at[here], flags_in, load_sem.at[4]),
        pltpu.make_async_copy(start_ref.at[here], own.at[0, core], load_sem.at[5]),
    ]
    for load in loads:
        load.start()
    row8 = lax.broadcasted_iota(jnp.int32, (ROWS, LANES), 0)
    lane = lax.broadcasted_iota(jnp.int32, (ROWS, LANES), 1)
    first_row, last_row = row8 == 0, row8 == ROWS - 1
    first_lane, last_lane = lane == 0, lane == LANES - 1
    row24 = lax.broadcasted_iota(jnp.int32, (EXT, LANES), 0)
    lane24 = lax.broadcasted_iota(jnp.int32, (EXT, LANES), 1)
    first24, last24 = lane24 == 0, lane24 == LANES - 1
    edge_valid = (last_row & has_above) | (first_row & has_below)
    valid24 = ((row24 >= ROWS) | has_above) & ((row24 < 2 * ROWS) | has_below)
    zero = jnp.zeros((ROWS, LANES), jnp.float32)
    for h in range(2):
        for pad in (pl.ds(0, ROWS), pl.ds(ROWS + EXT, ROWS)):
            mean_pad[h, pad] = zero
            for turn in range(2):
                for slot in range(group):
                    for i in range(2):
                        work[turn, slot, i, h, pad] = zero
    for load in loads:
        load.wait()

    inside_own = (flags_in[...] != 0).astype(jnp.float32)
    boost = 1.0 + (flags_in[...] == 2).astype(jnp.float32)
    cst_own = inside_own * boost * rate_in[...]
    bed_own = bed_in[...]
    for i, value in enumerate((cst_own, bed_own, inside_own)):
        stat_send[i] = value
        stat[i, core, ROWS : 2 * ROWS] = value

    pl.semaphore_wait(barrier, levels - 1 + 5)

    def scatter(src, dst, ssem, rsem):
        for peer in peers:
            rows_to = pl.ds(pl.multiple_of(tile_of(sx, peer) * ROWS, ROWS), ROWS)
            send(src.at[rows_to], dst, ssem, rsem, (peer, sx, core))

    scatter(guess, own.at[1 + level, core], gsend, grecv)
    scatter(balance, mass.at[level], bsend, brecv)
    around(stat_send, lambda p: stat.at[:, core, pl.ds(p * ROWS, ROWS)], ssend, srecv)
    own[1 + level, core] = guess[here]
    mass[level] = balance[here]

    wait(grecv, levels - 1)
    mine = own.at[pl.ds(1, levels), core]
    send(mine, mine, hsend, hrecv, (level, sx, other))
    for l in range(levels):
        row_send[0, l : l + 1] = own[1 + l, core, 0:1]
        row_send[1, l : l + 1] = own[1 + l, core, ROWS - 1 : ROWS]
    send(row_send.at[0], rows.at[1], esend, erecv, (above_tm, above_sx, core))
    send(row_send.at[1], rows.at[0], esend, erecv, (below_tm, below_sx, core))

    def neighbours(x, x_other, x_edge):
        right = pltpu.roll(jnp.where(first_lane, jnp.where(core == 0, x_other, 0.0), x), LANES - 1, 1)
        left = pltpu.roll(jnp.where(last_lane, jnp.where(core == 1, x_other, 0.0), x), 1, 1)
        down = pltpu.roll(jnp.where(first_row, x_edge, x), ROWS - 1, 0)
        up = pltpu.roll(jnp.where(last_row, x_edge, x), 1, 0)
        return right, left, down, up

    wait(srecv, 3 * 5)
    wait(erecv, 2 * (levels // ROWS))
    for l in range(levels):
        edge[l] = jnp.where(last_row, rows[0, l : l + 1], rows[1, l : l + 1])

    cst_other = stat[0, other, ROWS : 2 * ROWS]
    bed_other = stat[1, other, ROWS : 2 * ROWS]
    cst_edge = jnp.where(
        edge_valid, jnp.where(last_row, stat[0, core, 0:ROWS], stat[0, core, 2 * ROWS :]), 0.0
    )
    bed_edge = jnp.where(last_row, stat[1, core, 0:ROWS], stat[1, core, 2 * ROWS :])

    wait(hrecv, levels)

    def diffusivity(scale, h):
        return scale * h * h * jnp.abs(h)

    def newton(n, carry):
        more = n < NEWTON - 1

        sums = [zero, zero, zero]
        for l in range(levels):
            sums[0] = sums[0] + diffusivity(cst_own, own[1 + l, core])
            sums[1] = sums[1] + diffusivity(cst_other, own[1 + l, other])
            sums[2] = sums[2] + diffusivity(cst_edge, edge[l])
        mean, mean_other, mean_edge = (s * (1.0 / levels) for s in sums)
        total = 0.5 * (4.0 * mean + sum(neighbours(mean, mean_other, mean_edge)))
        for i, value in enumerate((mean, total)):
            dsend[n, i] = value
            dext[n, i, core, ROWS : 2 * ROWS] = value
        around(
            dsend.at[n], lambda p: dext.at[n, :, core, pl.ds(p * ROWS, ROWS)],
            dsem_s.at[n], dsem_r.at[n],
        )

        @pl.when(n == 0)
        def _():
            wait(brecv, levels - 1)

        for l in range(levels):
            h, h_other, h_edge = own[1 + l, core], own[1 + l, other], edge[l]
            s = h + bed_own
            d_near = neighbours(
                diffusivity(cst_own, h), diffusivity(cst_other, h_other),
                diffusivity(cst_edge, h_edge),
            )
            s_near = neighbours(
                s, h_other + bed_other, jnp.where(edge_valid, h_edge + bed_edge, 0.0)
            )
            d = diffusivity(cst_own, h)
            flux = sum((d + dn) * (s - sn) for dn, sn in zip(d_near, s_near))
            change = (h - own[l, core]) / time_step + 0.5 * flux - mass[l]
            resid[l] = inside_own * change * (root ** l)

        low = [resid[l] for l in range(half)]
        high = [resid[l + half] for l in range(half)]
        evens = forward_modes([a + b for a, b in zip(low, high)], half, levels, False)
        odds = forward_modes([a - b for a, b in zip(low, high)], half, levels, True)
        for slot in range(slots):
            for i in range(2):
                ysend[n, 0, 2 * slot + i] = evens[slot][i]
                ysend[n, 1, 2 * slot + i] = odds[slot][i]
                yext[n, 2 * slot + i, core, ROWS : 2 * ROWS] = jnp.where(
                    core == 0, evens[slot][i], odds[slot][i]
                )
            pair = pl.ds(2 * slot, 2)

            def place(p):
                return yext.at[n, pair, core, pl.ds(p * ROWS, ROWS)]

            s_sem, r_sem = ysem_s.at[n], ysem_r.at[n, slot]
            for to in range(2):
                send(ysend.at[n, to, pair], place(2), s_sem, r_sem, (above_tm, above_sx, to))
                send(ysend.at[n, to, pair], place(0), s_sem, r_sem, (below_tm, below_sx, to))
            send(ysend.at[n, other, pair], place(1), s_sem, r_sem, (level, sx, other))

        wait(dsem_r.at[n], 2 * 5)
        inner = pl.ds(ROWS, EXT)
        m0, m1 = (jnp.where(valid24, dext[n, 0, h], 0.0) for h in range(2))
        mean_pad[0, inner] = m0
        mean_pad[1, inner] = m1
        weight[0, 0] = 0.5 * (m0 + pltpu.roll(jnp.where(first24, m1, m0), LANES - 1, 1))
        weight[0, 1] = jnp.where(last24, 0.0, 0.5 * (m1 + pltpu.roll(m1, LANES - 1, 1)))
        weight[1, 0] = jnp.where(first24, 0.0, 0.5 * (m0 + pltpu.roll(m0, 1, 1)))
        weight[1, 1] = 0.5 * (m1 + pltpu.roll(jnp.where(last24, m0, m1), 1, 1))
        for h, m in ((0, m0), (1, m1)):
            weight[2, h] = 0.5 * (m + mean_pad[h, pl.ds(ROWS + 1, EXT)])
            weight[3, h] = 0.5 * (m + mean_pad[h, pl.ds(ROWS - 1, EXT)])

        def shift(k):
            angle = 2 * math.pi * k / levels
            return (
                (1.0 - root * math.cos(angle)) / time_step,
                root * math.sin(angle) / time_step,
            )

        for m in range(slots):
            even_real, even_imag = shift(2 * m)
            odd_real, odd_imag = shift(2 * m + 1)
            last_real = shift(half)[0] if m == 0 else even_real
            imag = jnp.where(core == 0, 0.0 if m == 0 else even_imag, odd_imag)
            for h in range(2):
                inside = jnp.where(valid24, stat[2, h], 0.0)
                real = dext[n, 1, h] + jnp.where(core == 0, even_real, odd_real)
                scaled = inside / (real * real + imag * imag)
                coef[m, 0, h] = scaled * real
                coef[m, 1, h] = scaled * -imag
                if m == 0:
                    real = dext[n, 1, h] + jnp.where(core == 0, last_real, odd_real)
                    coef[m, 2, h] = inside * real / (real * real + imag * imag)
                else:
                    coef[m, 2, h] = scaled * real

        def solve(g, carry):
            for i in range(group):
                wait(ysem_r.at[n, g * group + i], 2 * 5)

            def apply(slot, h, real, imag):
                a, b, c = (coef[slot, k, h] for k in range(3))
                return real * a - imag * b, real * b + imag * c

            for i in range(group):
                slot = g * group + i
                for h in range(2):
                    value = apply(slot, h, yext[n, 2 * slot, h], yext[n, 2 * slot + 1, h])
                    for part in range(2):
                        work[0, i, part, h, inner] = value[part]
            for sweep in range(SWEEPS - 1):
                now, then = sweep % 2, (sweep + 1) % 2
                for i in range(group):
                    slot = g * group + i
                    spread = []
                    for part in range(2):
                        v0, v1 = work[now, i, part, 0, inner], work[now, i, part, 1, inner]
                        right = (
                            pltpu.roll(jnp.where(first24, v1, v0), LANES - 1, 1),
                            pltpu.roll(v1, LANES - 1, 1),
                        )
                        left = (
                            pltpu.roll(v0, 1, 1),
                            pltpu.roll(jnp.where(last24, v0, v1), 1, 1),
                        )
                        spread.append([
                            weight[0, h] * right[h] + weight[1, h] * left[h]
                            + weight[2, h] * work[now, i, part, h, pl.ds(ROWS + 1, EXT)]
                            + weight[3, h] * work[now, i, part, h, pl.ds(ROWS - 1, EXT)]
                            for h in range(2)
                        ])
                    for h in range(2):
                        value = apply(
                            slot, h, yext[n, 2 * slot, h] + spread[0][h],
                            yext[n, 2 * slot + 1, h] + spread[1][h],
                        )
                        for part in range(2):
                            v = value[part]
                            if sweep < SWEEPS - 2:
                                work[then, i, part, h, inner] = v
                            else:
                                modes[h, 2 * slot + part] = v[ROWS : 2 * ROWS]
                                modes[2 + h, 2 * slot + part] = jnp.where(
                                    last_row, v[0:ROWS], v[2 * ROWS :]
                                )
            return carry

        lax.fori_loop(0, slots // group, solve, 0)

        for parity in range(2):
            @pl.when(core == parity)
            def _():
                def invert(i, carry):
                    p = (i & 2) + jnp.where((i & 1) == 0, other, core)
                    values = inverse_modes(
                        [modes[p, f] for f in range(half)], half, levels, parity == 1
                    )
                    for l in range(half):
                        parts[n, parity, p, l] = values[l]
                    block = parts.at[n, parity, p]

                    @pl.when(i == 0)
                    def _():
                        send(block, block, psem_s.at[n], psem_r.at[n], (level, sx, other))

                    @pl.when((i > 0) & (i < 3) & more)
                    def _():
                        send(block, block, qsem_s, qsem_r, (level, sx, other))

                    return carry

                lax.fori_loop(0, jnp.where(more, 4, 2), invert, 0)

        @pl.when(n == 0)
        def _():
            wait(hsend, levels)

        def update(target, p):
            for l in range(half):
                drop = root ** -l
                even, odd = parts[n, 0, p, l], parts[n, 1, p, l]
                near, far = target(l), target(l + half)
                near[...] = near[...] - (even + odd) * drop
                far[...] = far[...] - (even - odd) * (drop * root ** -half)

        wait(psem_r.at[n], half)
        update(lambda l: own.at[1 + l, core], core)

        @pl.when(more)
        def _():
            wait(qsem_r, 2 * half)
            update(lambda l: own.at[1 + l, other], other)
            update(lambda l: edge.at[l], 2 + core)

        return carry

    lax.fori_loop(0, NEWTON, newton, 0)

    for peer in peers:
        send(own.at[1 + peer, core], out_ref.at[0, here], osend, orecv, (peer, sx, core))
    out_ref[0, here] = own[1 + level, core]

    wait(gsend, levels - 1)
    wait(bsend, levels - 1)
    wait(ssend, 3 * 5)
    wait(esend, 2 * (levels // ROWS))
    for n in range(NEWTON):
        wait(dsem_s.at[n], 2 * 5)
        wait(ysem_s.at[n], 2 * 5 * slots)
        wait(psem_s.at[n], half)
    if NEWTON > 1:
        wait(qsem_s, 2 * half * (NEWTON - 1))
    wait(osend, levels - 1)
    wait(orecv, levels - 1)


def solution(mesh):
    levels, stripes = mesh.shape["tm"], mesh.shape["sx"]
    half = levels // 2
    slots = half // 2
    tile = (ROWS, LANES)
    wide = (EXT, LANES)
    padded = (EXT + 2 * ROWS, LANES)
    f32 = jnp.float32

    def vmem(*lead, last=tile, dtype=f32):
        return pltpu.VMEM((*lead, *last), dtype)

    dma = pltpu.SemaphoreType.DMA

    def body(guess, start, bed, rate, balance, flags):
        rows = guess.shape[1]
        return pl.pallas_call(
            functools.partial(kernel, levels, stripes),
            out_shape=jax.ShapeDtypeStruct(guess.shape, f32),
            in_specs=[pl.BlockSpec(memory_space=pl.ANY)] * 6,
            out_specs=pl.BlockSpec(memory_space=pltpu.VMEM),
            scratch_shapes=[
                vmem(last=(rows, LANES)), vmem(last=(rows, LANES)),
                vmem(), vmem(), vmem(dtype=jnp.int32),
                vmem(levels + 1, 2), vmem(levels), vmem(levels),
                vmem(3), vmem(3, 2, last=wide),
                vmem(2, last=(levels, LANES)), vmem(2, last=(levels, LANES)),
                vmem(NEWTON, 2), vmem(NEWTON, 2, 2, last=wide),
                vmem(levels), vmem(NEWTON, 2, half),
                vmem(NEWTON, half, 2, last=wide),
                vmem(slots, 3, 2, last=wide), vmem(2, last=padded), vmem(4, 2, last=wide),
                vmem(2, min(GROUP, slots), 2, 2, last=padded),
                vmem(4, half), vmem(NEWTON, 2, 4, half),
                vmem(max(2 * 5 * slots, 4 * half, levels)),
                dma((6,)), dma, dma, dma, dma, dma, dma, dma, dma,
                dma, dma, dma, dma, dma((NEWTON,)), dma((NEWTON,)),
                dma((NEWTON,)), dma((NEWTON, slots)), dma((NEWTON,)), dma((NEWTON,)), dma, dma,
            ],
            compiler_params=pltpu.CompilerParams(collective_id=0, has_side_effects=True),
        )(guess, start, bed, rate, balance, flags)

    return jax.shard_map(
        body, mesh=mesh,
        in_specs=(
            P("tm", "sx", "sy"), P("sx", "sy"), P("sx", "sy"), P("sx", "sy"),
            P("tm", "sx", "sy"), P("sx", "sy"),
        ),
        out_specs=P("tm", "sx", "sy"), check_vma=False,
    )
```

time: 55.3 us -> 43.4 us (0.78)
  Pallas kernels: 53.6 us -> 41.7 us
    pallas_call x1, Pallas kernels: 53.6 us -> 41.7 us  [body(): pl.pallas_call(functools.partial(kernel, levels, stripes), out_shape=jax....]
where the time goes in v2:
time: 43.4 us; the launch traced here: 43.3 us
  Pallas kernels  41.7 us (96%)
  local copies, waits for them, and re-layouts  1.57 us (4%)
    pallas_call x1, Pallas kernels, body(): pl.pallas_call(functools.partial(kernel, levels, stripes), out_shape=jax....  41.7 us
    unnamed x1, local copies, waits for them, and re-layouts  1.57 us

profile of v2, /device:TPU:6, one launch (start us, length us, event | category | flops | bytes accessed | tf_op | source)
XLA Modules:
  0.0 43.3 jit_solution(13235291706827432856)
XLA Ops:
  0.0 41.7 %shard_map.64 = f32[1,256,128]{2,1,0:T(8,128)} custom-call(f32[1,256,128]{2,1,0:T(8,128)} %guess_ref.1, f32[256,128]{1,0:T(8,128)} %start_ref.1, f32[256,128]{1,0:T(8,128)} %bed_ref.1, f32[256,128]{1,0:T(8,128)} %rate_ref.1, f32[1,256,128]{2,1,0:T(8,128)} %balance_ref.1, s32[256,128]{1,0:T(8,128)} %flags_ref.1), custom_call_target="tpu_custom_call" | custom-call | tf_op jit(solution)/shard_map/pallas_call | solution.py:488
  41.7 1.6 %copy.8 = f32[1,256,128]{2,1,0:T(8,128)} copy(f32[1,256,128]{2,1,0:T(8,128)} %shard_map.64) | data formatting | bytes 262144

commit v3 on v2

--- a/solution.py
+++ b/solution.py
@@ -487,7 +487,7 @@
         rows = guess.shape[1]
         return pl.pallas_call(
             functools.partial(kernel, levels, stripes),
-            out_shape=jax.ShapeDtypeStruct(guess.shape, f32),
+            out_shape=pltpu.VMEM(guess.shape, f32),
             in_specs=[pl.BlockSpec(memory_space=pl.ANY)] * 6,
             out_specs=pl.BlockSpec(memory_space=pltpu.VMEM),
             scratch_shapes=[

time: 43.4 us -> 41.8 us (0.963)
  local copies, waits for them, and re-layouts: 1.57 us -> 0.66 us
  Pallas kernels: 41.7 us -> 41 us
    unnamed x1, local copies, waits for them, and re-layouts: 1.57 us -> 0.66 us
    pallas_call x1, Pallas kernels: 41.7 us -> 41 us  [body(): pl.pallas_call(functools.partial(kernel, levels, stripes), out_shape=pltp...]
where the time goes in v3:
time: 41.8 us; the launch traced here: 41.7 us
  Pallas kernels  41 us (98%)
  local copies, waits for them, and re-layouts  0.66 us (2%)
    pallas_call x1, Pallas kernels, body(): pl.pallas_call(functools.partial(kernel, levels, stripes), out_shape=pltp...  41 us

profile of v3, /device:TPU:6, one launch (start us, length us, event | category | flops | bytes accessed | tf_op | source)
XLA Modules:
  0.0 41.7 jit_solution(8335883372390170168)
XLA Ops:
  0.0 41.0 %shard_map.64 = f32[1,256,128]{2,1,0:T(8,128)S(1)} custom-call(f32[1,256,128]{2,1,0:T(8,128)} %guess_ref.1, f32[256,128]{1,0:T(8,128)} %start_ref.1, f32[256,128]{1,0:T(8,128)} %bed_ref.1, f32[256,128]{1,0:T(8,128)} %rate_ref.1, f32[1,256,128]{2,1,0:T(8,128)} %balance_ref.1, s32[256,128]{1,0:T(8,128)} %flags_ref.1), custom_call_target="tpu_custom_call" | custom-call | tf_op jit(solution)/shard_map/pallas_call | solution.py:488
  41.1 0.7 %copy.8 = f32[1,256,128]{2,1,0:T(8,128)} copy(f32[1,256,128]{2,1,0:T(8,128)S(1)} %shard_map.64) | data formatting | bytes 262144

commit v4 on v3

--- a/solution.py
+++ b/solution.py
@@ -15,6 +15,7 @@
 LANES = 128
 EXT = 3 * ROWS
 GROUP = 4
+CHUNK = 4
 
 circulant_weight = 0.25
 time_step = 1.0
@@ -93,7 +94,7 @@
     guess_ref, start_ref, bed_ref, rate_ref, balance_ref, flags_ref,
     out_ref,
     guess, balance, bed_in, rate_in, flags_in,
-    own, edge, mass, stat_send, stat, row_send, rows,
+    own, edge, mass, stat_send, stat, row_send, rows, row_dummy,
     dsend, dext, resid, ysend, yext, coef, mean_pad, weight, work, modes, parts, dummy,
     load_sem, gsend, grecv, bsend, brecv, ssend, srecv, osend, orecv,
     esend, erecv, hsend, hrecv, dsem_s, dsem_r, ysem_s, ysem_r,
@@ -105,6 +106,7 @@
     tiles = stripes * levels
     root = circulant_weight ** (1.0 / levels)
     group = min(GROUP, slots)
+    chunk = min(CHUNK, group)
 
     level = lax.axis_index("tm")
     sx = lax.axis_index("sx")
@@ -150,6 +152,10 @@
         view = dummy.at[pl.ds(0, count)]
         pltpu.make_async_copy(view, view, sem).wait()
 
+    def wait_rows(sem, count):
+        view = row_dummy.at[pl.ds(0, count)]
+        pltpu.make_async_copy(view, view, sem).wait()
+
     def around(src, place, ssem, rsem):
         for to in range(2):
             send(src, place(2), ssem, rsem, (above_tm, above_sx, to))
@@ -167,6 +173,18 @@
     for to in range(2):
         greet((above_tm, above_sx, to))
         greet((below_tm, below_sx, to))
+
+    next_sx = (sx + 1) & (stripes - 1)
+    prev_sx = (sx + stripes - 1) & (stripes - 1)
+    at_start, at_end = tile == 0, tile == levels - 1
+    for at, stripe in ((at_start, prev_sx), (at_end, next_sx)):
+        @pl.when(at)
+        def _():
+            def tell(tm, carry):
+                greet((tm, stripe, core))
+                return carry
+
+            lax.fori_loop(0, levels, tell, 0)
 
     here = pl.ds(pl.multiple_of(tile * ROWS, ROWS), ROWS)
     loads = [
@@ -207,7 +225,11 @@
         stat_send[i] = value
         stat[i, core, ROWS : 2 * ROWS] = value
 
-    pl.semaphore_wait(barrier, levels - 1 + 5)
+    for t in range(levels):
+        row_send[0, t] = guess[t * ROWS + ROWS - 1 : t * ROWS + ROWS]
+        row_send[1, t] = guess[t * ROWS : t * ROWS + 1]
+
+    pl.semaphore_wait(barrier, levels - 1 + 5 + 2)
 
     def scatter(src, dst, ssem, rsem):
         for peer in peers:
@@ -215,6 +237,34 @@
             send(src.at[rows_to], dst, ssem, rsem, (peer, sx, core))
 
     scatter(guess, own.at[1 + level, core], gsend, grecv)
+    for peer in peers:
+        to = tile_of(sx, peer)
+
+        @pl.when(to > 0)
+        def _():
+            send(row_send.at[0, to - 1], rows.at[0, level], esend, erecv, (peer, sx, core))
+
+        @pl.when(to < levels - 1)
+        def _():
+            send(row_send.at[1, to + 1], rows.at[1, level], esend, erecv, (peer, sx, core))
+
+    send(
+        row_send.at[0, levels - 1], rows.at[0, level], esend, erecv,
+        (owner_of(next_sx, 0), next_sx, core),
+    )
+    send(
+        row_send.at[1, 0], rows.at[1, level], esend, erecv,
+        (owner_of(prev_sx, levels - 1), prev_sx, core),
+    )
+
+    @pl.when(tile > 0)
+    def _():
+        rows[0, level] = row_send[0, tile - 1]
+
+    @pl.when(tile < levels - 1)
+    def _():
+        rows[1, level] = row_send[1, tile + 1]
+
     scatter(balance, mass.at[level], bsend, brecv)
     around(stat_send, lambda p: stat.at[:, core, pl.ds(p * ROWS, ROWS)], ssend, srecv)
     own[1 + level, core] = guess[here]
@@ -223,11 +273,6 @@
     wait(grecv, levels - 1)
     mine = own.at[pl.ds(1, levels), core]
     send(mine, mine, hsend, hrecv, (level, sx, other))
-    for l in range(levels):
-        row_send[0, l : l + 1] = own[1 + l, core, 0:1]
-        row_send[1, l : l + 1] = own[1 + l, core, ROWS - 1 : ROWS]
-    send(row_send.at[0], rows.at[1], esend, erecv, (above_tm, above_sx, core))
-    send(row_send.at[1], rows.at[0], esend, erecv, (below_tm, below_sx, core))
 
     def neighbours(x, x_other, x_edge):
         right = pltpu.roll(jnp.where(first_lane, jnp.where(core == 0, x_other, 0.0), x), LANES - 1, 1)
@@ -237,9 +282,17 @@
         return right, left, down, up
 
     wait(srecv, 3 * 5)
-    wait(erecv, 2 * (levels // ROWS))
+
+    @pl.when(at_start | at_end)
+    def _():
+        wait_rows(erecv, 2 * levels - 1)
+
+    @pl.when(jnp.logical_not(at_start | at_end))
+    def _():
+        wait_rows(erecv, 2 * levels - 2)
+
     for l in range(levels):
-        edge[l] = jnp.where(last_row, rows[0, l : l + 1], rows[1, l : l + 1])
+        edge[l] = jnp.where(last_row, rows[0, l], rows[1, l])
 
     cst_other = stat[0, other, ROWS : 2 * ROWS]
     bed_other = stat[1, other, ROWS : 2 * ROWS]
@@ -301,12 +354,14 @@
                 yext[n, 2 * slot + i, core, ROWS : 2 * ROWS] = jnp.where(
                     core == 0, evens[slot][i], odds[slot][i]
                 )
-            pair = pl.ds(2 * slot, 2)
+            if slot % chunk != chunk - 1:
+                continue
+            pair = pl.ds(2 * (slot + 1 - chunk), 2 * chunk)
 
             def place(p):
                 return yext.at[n, pair, core, pl.ds(p * ROWS, ROWS)]
 
-            s_sem, r_sem = ysem_s.at[n], ysem_r.at[n, slot]
+            s_sem, r_sem = ysem_s.at[n], ysem_r.at[n, slot // chunk]
             for to in range(2):
                 send(ysend.at[n, to, pair], place(2), s_sem, r_sem, (above_tm, above_sx, to))
                 send(ysend.at[n, to, pair], place(0), s_sem, r_sem, (below_tm, below_sx, to))
@@ -350,54 +405,64 @@
                     coef[m, 2, h] = scaled * real
 
         def solve(g, carry):
+            for i in range(group // chunk):
+                wait(ysem_r.at[n, g * (group // chunk) + i], 2 * 5 * chunk)
+
+            def apply(i, h, t, real, imag):
+                rows_t = slice(t * ROWS, (t + 1) * ROWS)
+                a, b = (coef[g * group + i, k, h, rows_t] for k in range(2))
+                c = coef[g * group, 2, h, rows_t] if i == 0 else a
+                return real * a - imag * b, real * b + imag * c
+
+            def source(i, part, h, t):
+                return yext[n, 2 * (g * group + i) + part, h, t * ROWS : (t + 1) * ROWS]
+
+            blocks = [(h, t) for h in range(2) for t in range(EXT // ROWS)]
             for i in range(group):
-                wait(ysem_r.at[n, g * group + i], 2 * 5)
-
-            def apply(slot, h, real, imag):
-                a, b, c = (coef[slot, k, h] for k in range(3))
-                return real * a - imag * b, real * b + imag * c
-
-            for i in range(group):
-                slot = g * group + i
-                for h in range(2):
-                    value = apply(slot, h, yext[n, 2 * slot, h], yext[n, 2 * slot + 1, h])
+                for h, t in blocks:
+                    value = apply(i, h, t, source(i, 0, h, t), source(i, 1, h, t))
                     for part in range(2):
-                        work[0, i, part, h, inner] = value[part]
+                        work[0, i, part, h, pl.ds(ROWS * (1 + t), ROWS)] = value[part]
             for sweep in range(SWEEPS - 1):
                 now, then = sweep % 2, (sweep + 1) % 2
-                for i in range(group):
-                    slot = g * group + i
-                    spread = []
-                    for part in range(2):
-                        v0, v1 = work[now, i, part, 0, inner], work[now, i, part, 1, inner]
-                        right = (
-                            pltpu.roll(jnp.where(first24, v1, v0), LANES - 1, 1),
-                            pltpu.roll(v1, LANES - 1, 1),
-                        )
-                        left = (
-                            pltpu.roll(v0, 1, 1),
-                            pltpu.roll(jnp.where(last24, v0, v1), 1, 1),
-                        )
-                        spread.append([
-                            weight[0, h] * right[h] + weight[1, h] * left[h]
-                            + weight[2, h] * work[now, i, part, h, pl.ds(ROWS + 1, EXT)]
-                            + weight[3, h] * work[now, i, part, h, pl.ds(ROWS - 1, EXT)]
-                            for h in range(2)
-                        ])
-                    for h in range(2):
-                        value = apply(
-                            slot, h, yext[n, 2 * slot, h] + spread[0][h],
-                            yext[n, 2 * slot + 1, h] + spread[1][h],
-                        )
+                for first in range(0, group, 2):
+                    pair = range(first, min(first + 2, group))
+                    right, left, last = {}, {}, {}
+                    for i in pair:
                         for part in range(2):
-                            v = value[part]
-                            if sweep < SWEEPS - 2:
-                                work[then, i, part, h, inner] = v
-                            else:
-                                modes[h, 2 * slot + part] = v[ROWS : 2 * ROWS]
-                                modes[2 + h, 2 * slot + part] = jnp.where(
-                                    last_row, v[0:ROWS], v[2 * ROWS :]
-                                )
+                            v0, v1 = work[now, i, part, 0, inner], work[now, i, part, 1, inner]
+                            right[i, part] = (
+                                pltpu.roll(jnp.where(first24, v1, v0), LANES - 1, 1),
+                                pltpu.roll(v1, LANES - 1, 1),
+                            )
+                            left[i, part] = (
+                                pltpu.roll(v0, 1, 1),
+                                pltpu.roll(jnp.where(last24, v0, v1), 1, 1),
+                            )
+                    for h, t in blocks:
+                        rows_t = slice(t * ROWS, (t + 1) * ROWS)
+                        w = [weight[k, h, rows_t] for k in range(4)]
+                        for i in pair:
+                            total_t = [
+                                source(i, part, h, t)
+                                + w[0] * right[i, part][h][rows_t]
+                                + w[1] * left[i, part][h][rows_t]
+                                + w[2] * work[now, i, part, h, pl.ds(ROWS * (1 + t) + 1, ROWS)]
+                                + w[3] * work[now, i, part, h, pl.ds(ROWS * (1 + t) - 1, ROWS)]
+                                for part in range(2)
+                            ]
+                            value = apply(i, h, t, *total_t)
+                            for part in range(2):
+                                if sweep < SWEEPS - 2:
+                                    work[then, i, part, h, pl.ds(ROWS * (1 + t), ROWS)] = value[part]
+                                else:
+                                    last[i, part, h, t] = value[part]
+                    for (i, part, h, t), v in last.items():
+                        field = 2 * (g * group + i) + part
+                        if t == 1:
+                            modes[h, field] = v
+                        elif t == 2:
+                            modes[2 + h, field] = jnp.where(last_row, last[i, part, h, 0], v)
             return carry
 
         lax.fori_loop(0, slots // group, solve, 0)
@@ -458,7 +523,15 @@
     wait(gsend, levels - 1)
     wait(bsend, levels - 1)
     wait(ssend, 3 * 5)
-    wait(esend, 2 * (levels // ROWS))
+
+    @pl.when(at_start | at_end)
+    def _():
+        wait_rows(esend, 2 * levels - 1)
+
+    @pl.when(jnp.logical_not(at_start | at_end))
+    def _():
+        wait_rows(esend, 2 * levels - 2)
+
     for n in range(NEWTON):
         wait(dsem_s.at[n], 2 * 5)
         wait(ysem_s.at[n], 2 * 5 * slots)
@@ -495,7 +568,8 @@
                 vmem(), vmem(), vmem(dtype=jnp.int32),
                 vmem(levels + 1, 2), vmem(levels), vmem(levels),
                 vmem(3), vmem(3, 2, last=wide),
-                vmem(2, last=(levels, LANES)), vmem(2, last=(levels, LANES)),
+                vmem(2, levels, last=(1, LANES)), vmem(2, levels, last=(1, LANES)),
+                vmem(2 * levels, last=(1, LANES)),
                 vmem(NEWTON, 2), vmem(NEWTON, 2, 2, last=wide),
                 vmem(levels), vmem(NEWTON, 2, half),
                 vmem(NEWTON, half, 2, last=wide),

time: 41.8 us -> 41.1 us (0.983)
  Pallas kernels: 41 us -> 40.3 us
    pallas_call x1, Pallas kernels: 41 us -> 40.3 us  [body(): pl.pallas_call(functools.partial(kernel, levels, stripes), out_shape=pltp...]
where the time goes in v4:
time: 41.1 us; the launch traced here: 41 us
  Pallas kernels  40.3 us (98%)
  local copies, waits for them, and re-layouts  0.66 us (2%)
    pallas_call x1, Pallas kernels, body(): pl.pallas_call(functools.partial(kernel, levels, stripes), out_shape=pltp...  40.3 us

profile of v4, /device:TPU:6, one launch (start us, length us, event | category | flops | bytes accessed | tf_op | source)
XLA Modules:
  0.0 41.0 jit_solution(6978367453842165225)
XLA Ops:
  0.0 40.3 %shard_map.64 = f32[1,256,128]{2,1,0:T(8,128)S(1)} custom-call(f32[1,256,128]{2,1,0:T(8,128)} %guess_ref.1, f32[256,128]{1,0:T(8,128)} %start_ref.1, f32[256,128]{1,0:T(8,128)} %bed_ref.1, f32[256,128]{1,0:T(8,128)} %rate_ref.1, f32[1,256,128]{2,1,0:T(8,128)} %balance_ref.1, s32[256,128]{1,0:T(8,128)} %flags_ref.1), custom_call_target="tpu_custom_call" | custom-call | tf_op jit(solution)/shard_map/pallas_call | solution.py:561
  40.3 0.7 %copy.8 = f32[1,256,128]{2,1,0:T(8,128)} copy(f32[1,256,128]{2,1,0:T(8,128)S(1)} %shard_map.64) | data formatting | bytes 262144

commit v5 on v4

--- a/solution.py
+++ b/solution.py
@@ -14,8 +14,7 @@
 ROWS = 8
 LANES = 128
 EXT = 3 * ROWS
-GROUP = 4
-CHUNK = 4
+GROUPS = (4, 4)
 
 circulant_weight = 0.25
 time_step = 1.0
@@ -94,10 +93,10 @@
     guess_ref, start_ref, bed_ref, rate_ref, balance_ref, flags_ref,
     out_ref,
     guess, balance, bed_in, rate_in, flags_in,
-    own, edge, mass, stat_send, stat, row_send, rows, row_dummy,
+    own, edge, mass, stat_send, stat, row_send, rows, rows_far, row_dummy,
     dsend, dext, resid, ysend, yext, coef, mean_pad, weight, work, modes, parts, dummy,
     load_sem, gsend, grecv, bsend, brecv, ssend, srecv, osend, orecv,
-    esend, erecv, hsend, hrecv, dsem_s, dsem_r, ysem_s, ysem_r,
+    esend, erecv, frecv, hsend, hrecv, dsem_s, dsem_r, ysem_s, ysem_r,
     psem_s, psem_r, qsem_s, qsem_r,
 ):
     half = levels // 2
@@ -105,8 +104,9 @@
     ring_z = levels // RING_Y
     tiles = stripes * levels
     root = circulant_weight ** (1.0 / levels)
-    group = min(GROUP, slots)
-    chunk = min(CHUNK, group)
+    groups = GROUPS if sum(GROUPS) == slots else (slots,)
+    starts = [sum(groups[:i]) for i in range(len(groups))]
+    most = max(groups)
 
     level = lax.axis_index("tm")
     sx = lax.axis_index("sx")
@@ -211,7 +211,7 @@
         for pad in (pl.ds(0, ROWS), pl.ds(ROWS + EXT, ROWS)):
             mean_pad[h, pad] = zero
             for turn in range(2):
-                for slot in range(group):
+                for slot in range(most):
                     for i in range(2):
                         work[turn, slot, i, h, pad] = zero
     for load in loads:
@@ -226,8 +226,9 @@
         stat[i, core, ROWS : 2 * ROWS] = value
 
     for t in range(levels):
-        row_send[0, t] = guess[t * ROWS + ROWS - 1 : t * ROWS + ROWS]
-        row_send[1, t] = guess[t * ROWS : t * ROWS + 1]
+        for i, row in enumerate((t * ROWS - 1, t * ROWS + ROWS)):
+            row = row % (levels * ROWS)
+            row_send[t, i] = guess[row : row + 1]
 
     pl.semaphore_wait(barrier, levels - 1 + 5 + 2)
 
@@ -238,32 +239,16 @@
 
     scatter(guess, own.at[1 + level, core], gsend, grecv)
     for peer in peers:
-        to = tile_of(sx, peer)
-
-        @pl.when(to > 0)
-        def _():
-            send(row_send.at[0, to - 1], rows.at[0, level], esend, erecv, (peer, sx, core))
-
-        @pl.when(to < levels - 1)
-        def _():
-            send(row_send.at[1, to + 1], rows.at[1, level], esend, erecv, (peer, sx, core))
-
+        send(row_send.at[tile_of(sx, peer)], rows.at[level], esend, erecv, (peer, sx, core))
     send(
-        row_send.at[0, levels - 1], rows.at[0, level], esend, erecv,
+        row_send.at[0, 0], rows_far.at[level], esend, frecv,
         (owner_of(next_sx, 0), next_sx, core),
     )
     send(
-        row_send.at[1, 0], rows.at[1, level], esend, erecv,
+        row_send.at[levels - 1, 1], rows_far.at[level], esend, frecv,
         (owner_of(prev_sx, levels - 1), prev_sx, core),
     )
-
-    @pl.when(tile > 0)
-    def _():
-        rows[0, level] = row_send[0, tile - 1]
-
-    @pl.when(tile < levels - 1)
-    def _():
-        rows[1, level] = row_send[1, tile + 1]
+    rows[level] = row_send[tile]
 
     scatter(balance, mass.at[level], bsend, brecv)
     around(stat_send, lambda p: stat.at[:, core, pl.ds(p * ROWS, ROWS)], ssend, srecv)
@@ -282,17 +267,16 @@
         return right, left, down, up
 
     wait(srecv, 3 * 5)
-
-    @pl.when(at_start | at_end)
-    def _():
-        wait_rows(erecv, 2 * levels - 1)
-
-    @pl.when(jnp.logical_not(at_start | at_end))
-    def _():
-        wait_rows(erecv, 2 * levels - 2)
+    wait_rows(erecv, 2 * (levels - 1))
+    for i, at in enumerate((at_start, at_end)):
+        @pl.when(at)
+        def _():
+            wait_rows(frecv, levels)
+            for l in range(levels):
+                rows[l, i] = rows_far[l]
 
     for l in range(levels):
-        edge[l] = jnp.where(last_row, rows[0, l], rows[1, l])
+        edge[l] = jnp.where(last_row, rows[l, 0], rows[l, 1])
 
     cst_other = stat[0, other, ROWS : 2 * ROWS]
     bed_other = stat[1, other, ROWS : 2 * ROWS]
@@ -354,14 +338,15 @@
                 yext[n, 2 * slot + i, core, ROWS : 2 * ROWS] = jnp.where(
                     core == 0, evens[slot][i], odds[slot][i]
                 )
-            if slot % chunk != chunk - 1:
+            if slot + 1 not in starts[1:] + [slots]:
                 continue
-            pair = pl.ds(2 * (slot + 1 - chunk), 2 * chunk)
+            index = max(i for i, start in enumerate(starts) if start <= slot)
+            pair = pl.ds(2 * starts[index], 2 * groups[index])
 
             def place(p):
                 return yext.at[n, pair, core, pl.ds(p * ROWS, ROWS)]
 
-            s_sem, r_sem = ysem_s.at[n], ysem_r.at[n, slot // chunk]
+            s_sem, r_sem = ysem_s.at[n], ysem_r.at[n, index]
             for to in range(2):
                 send(ysend.at[n, to, pair], place(2), s_sem, r_sem, (above_tm, above_sx, to))
                 send(ysend.at[n, to, pair], place(0), s_sem, r_sem, (below_tm, below_sx, to))
@@ -404,68 +389,70 @@
                 else:
                     coef[m, 2, h] = scaled * real
 
-        def solve(g, carry):
-            for i in range(group // chunk):
-                wait(ysem_r.at[n, g * (group // chunk) + i], 2 * 5 * chunk)
-
-            def apply(i, h, t, real, imag):
-                rows_t = slice(t * ROWS, (t + 1) * ROWS)
-                a, b = (coef[g * group + i, k, h, rows_t] for k in range(2))
-                c = coef[g * group, 2, h, rows_t] if i == 0 else a
+        for index, (start, group) in enumerate(zip(starts, groups)):
+            wait(ysem_r.at[n, index], 2 * 5 * group)
+
+            def apply(i, h, row, real, imag):
+                a, b = (coef[start + i, k, h, pl.ds(row, ROWS)] for k in range(2))
+                c = coef[0, 2, h, pl.ds(row, ROWS)] if start + i == 0 else a
                 return real * a - imag * b, real * b + imag * c
 
-            def source(i, part, h, t):
-                return yext[n, 2 * (g * group + i) + part, h, t * ROWS : (t + 1) * ROWS]
-
-            blocks = [(h, t) for h in range(2) for t in range(EXT // ROWS)]
+            def source(i, part, h, row):
+                return yext[n, 2 * (start + i) + part, h, pl.ds(row, ROWS)]
+
             for i in range(group):
-                for h, t in blocks:
-                    value = apply(i, h, t, source(i, 0, h, t), source(i, 1, h, t))
-                    for part in range(2):
-                        work[0, i, part, h, pl.ds(ROWS * (1 + t), ROWS)] = value[part]
+                for h in range(2):
+                    for row in range(0, EXT, ROWS):
+                        value = apply(i, h, row, source(i, 0, h, row), source(i, 1, h, row))
+                        for part in range(2):
+                            work[0, i, part, h, pl.ds(ROWS + row, ROWS)] = value[part]
             for sweep in range(SWEEPS - 1):
                 now, then = sweep % 2, (sweep + 1) % 2
+                base = ROWS // 2 if sweep + 1 >= ROWS // 2 else 0
+                span = EXT - 2 * base
+                window = pl.ds(ROWS + base, span)
                 for first in range(0, group, 2):
                     pair = range(first, min(first + 2, group))
-                    right, left, last = {}, {}, {}
+                    right, left = {}, {}
                     for i in pair:
                         for part in range(2):
-                            v0, v1 = work[now, i, part, 0, inner], work[now, i, part, 1, inner]
+                            v0, v1 = work[now, i, part, 0, window], work[now, i, part, 1, window]
                             right[i, part] = (
-                                pltpu.roll(jnp.where(first24, v1, v0), LANES - 1, 1),
+                                pltpu.roll(jnp.where(first24[:span], v1, v0), LANES - 1, 1),
                                 pltpu.roll(v1, LANES - 1, 1),
                             )
                             left[i, part] = (
                                 pltpu.roll(v0, 1, 1),
-                                pltpu.roll(jnp.where(last24, v0, v1), 1, 1),
+                                pltpu.roll(jnp.where(last24[:span], v0, v1), 1, 1),
                             )
-                    for h, t in blocks:
-                        rows_t = slice(t * ROWS, (t + 1) * ROWS)
-                        w = [weight[k, h, rows_t] for k in range(4)]
-                        for i in pair:
-                            total_t = [
-                                source(i, part, h, t)
-                                + w[0] * right[i, part][h][rows_t]
-                                + w[1] * left[i, part][h][rows_t]
-                                + w[2] * work[now, i, part, h, pl.ds(ROWS * (1 + t) + 1, ROWS)]
-                                + w[3] * work[now, i, part, h, pl.ds(ROWS * (1 + t) - 1, ROWS)]
-                                for part in range(2)
-                            ]
-                            value = apply(i, h, t, *total_t)
-                            for part in range(2):
-                                if sweep < SWEEPS - 2:
-                                    work[then, i, part, h, pl.ds(ROWS * (1 + t), ROWS)] = value[part]
-                                else:
-                                    last[i, part, h, t] = value[part]
-                    for (i, part, h, t), v in last.items():
-                        field = 2 * (g * group + i) + part
-                        if t == 1:
-                            modes[h, field] = v
-                        elif t == 2:
-                            modes[2 + h, field] = jnp.where(last_row, last[i, part, h, 0], v)
-            return carry
-
-        lax.fori_loop(0, slots // group, solve, 0)
+                    for h in range(2):
+                        for t in range(span // ROWS):
+                            row = base + t * ROWS
+                            rows_t = slice(t * ROWS, (t + 1) * ROWS)
+                            w = [weight[k, h, pl.ds(row, ROWS)] for k in range(4)]
+                            for i in pair:
+                                total_t = [
+                                    source(i, part, h, row)
+                                    + w[0] * right[i, part][h][rows_t]
+                                    + w[1] * left[i, part][h][rows_t]
+                                    + w[2] * work[now, i, part, h, pl.ds(ROWS + row + 1, ROWS)]
+                                    + w[3] * work[now, i, part, h, pl.ds(ROWS + row - 1, ROWS)]
+                                    for part in range(2)
+                                ]
+                                value = apply(i, h, row, *total_t)
+                                for part in range(2):
+                                    work[then, i, part, h, pl.ds(ROWS + row, ROWS)] = value[part]
+            final = (SWEEPS - 1) % 2
+            for i in range(group):
+                for part in range(2):
+                    for h in range(2):
+                        field = 2 * (start + i) + part
+                        modes[h, field] = work[final, i, part, h, pl.ds(2 * ROWS, ROWS)]
+                        modes[2 + h, field] = jnp.where(
+                            last_row,
+                            work[final, i, part, h, pl.ds(ROWS, ROWS)],
+                            work[final, i, part, h, pl.ds(3 * ROWS, ROWS)],
+                        )
 
         for parity in range(2):
             @pl.when(core == parity)
@@ -523,15 +510,7 @@
     wait(gsend, levels - 1)
     wait(bsend, levels - 1)
     wait(ssend, 3 * 5)
-
-    @pl.when(at_start | at_end)
-    def _():
-        wait_rows(esend, 2 * levels - 1)
-
-    @pl.when(jnp.logical_not(at_start | at_end))
-    def _():
-        wait_rows(esend, 2 * levels - 2)
-
+    wait_rows(esend, 2 * levels)
     for n in range(NEWTON):
         wait(dsem_s.at[n], 2 * 5)
         wait(ysem_s.at[n], 2 * 5 * slots)
@@ -568,16 +547,17 @@
                 vmem(), vmem(), vmem(dtype=jnp.int32),
                 vmem(levels + 1, 2), vmem(levels), vmem(levels),
                 vmem(3), vmem(3, 2, last=wide),
-                vmem(2, levels, last=(1, LANES)), vmem(2, levels, last=(1, LANES)),
+                vmem(levels, 2, last=(1, LANES)), vmem(levels, 2, last=(1, LANES)),
+                vmem(levels, last=(1, LANES)),
                 vmem(2 * levels, last=(1, LANES)),
                 vmem(NEWTON, 2), vmem(NEWTON, 2, 2, last=wide),
                 vmem(levels), vmem(NEWTON, 2, half),
                 vmem(NEWTON, half, 2, last=wide),
                 vmem(slots, 3, 2, last=wide), vmem(2, last=padded), vmem(4, 2, last=wide),
-                vmem(2, min(GROUP, slots), 2, 2, last=padded),
+                vmem(2, slots, 2, 2, last=padded),
                 vmem(4, half), vmem(NEWTON, 2, 4, half),
                 vmem(max(2 * 5 * slots, 4 * half, levels)),
-                dma((6,)), dma, dma, dma, dma, dma, dma, dma, dma,
+                dma((6,)), dma, dma, dma, dma, dma, dma, dma, dma, dma,
                 dma, dma, dma, dma, dma((NEWTON,)), dma((NEWTON,)),
                 dma((NEWTON,)), dma((NEWTON, slots)), dma((NEWTON,)), dma((NEWTON,)), dma, dma,
             ],

time: 41.1 us -> 41 us (level)
  no operation moved by 1% of the time
where the time goes in v5:
time: 41 us; the launch traced here: 40.6 us
  Pallas kernels  40 us (98%)
  local copies, waits for them, and re-layouts  0.66 us (2%)
    pallas_call x1, Pallas kernels, body(): pl.pallas_call(functools.partial(kernel, levels, stripes), out_shape=pltp...  40 us

profile of v5, /device:TPU:6, one launch (start us, length us, event | category | flops | bytes accessed | tf_op | source)
XLA Modules:
  0.0 40.6 jit_solution(14445014549810057243)
XLA Ops:
  0.0 40.0 %shard_map.64 = f32[1,256,128]{2,1,0:T(8,128)S(1)} custom-call(f32[1,256,128]{2,1,0:T(8,128)} %guess_ref.1, f32[256,128]{1,0:T(8,128)} %start_ref.1, f32[256,128]{1,0:T(8,128)} %bed_ref.1, f32[256,128]{1,0:T(8,128)} %rate_ref.1, f32[1,256,128]{2,1,0:T(8,128)} %balance_ref.1, s32[256,128]{1,0:T(8,128)} %flags_ref.1), custom_call_target="tpu_custom_call" | custom-call | tf_op jit(solution)/shard_map/pallas_call | solution.py:540
  40.0 0.7 %copy.8 = f32[1,256,128]{2,1,0:T(8,128)} copy(f32[1,256,128]{2,1,0:T(8,128)S(1)} %shard_map.64) | data formatting | bytes 262144
